TPU v7x, 768 devices: a whole 4x8x12 slice. The times are simulated.
768 devices in a mesh: pair: 32 (over y, x), grow: 8 (over z_lo, core), gcol: 3 (over z_hi).
Axes of the slice: x: 4, y: 8, z: 12 (z_hi: 3, z_lo: 4; z = z_hi * 4 + z_lo), core: 2. Of those that a mesh axis runs over, the one named last changes fastest.
Arguments:
- valence: bfloat16 [16, 96, 9216], P(None, 'grow'), may hold values from -6 to 6
- conduction: bfloat16 [192, 96, 9216], P(('pair', 'gcol'), 'grow'), may hold values from -6 to 6
- val_energy: float32 [16], replicated, may hold values from -10 to -1
- cond_energy: float32 [192], replicated, may hold values from 1 to 20
- val_occupation: int32 [16], replicated, may hold values from 1 to 16
- gvectors: int32 [3, 3840], replicated, may hold values from -12 to 12, as said below
Outputs:
- chi_zero: float32 [7680, 7680], P(('pair', 'gcol'), 'grow')
Inputs may be any that keep to these rules, and one draw needn't show every extreme that they name: gvectors holds 3840 distinct wave vectors; the first component lies in 1 .. 12, the other two in -12 .. 12.
All inputs are finite; a program needn't handle non-finite values.
Results may differ from a plain program's by a relative error of at most 0.02.
Values may be sent and summed in bfloat16 or wider, within the bound.
A program may use at most 64 MiB of HBM per device.

v0:
```python
import math

import jax
import jax.numpy as jnp
from jax import lax
from jax.sharding import Mesh
from jax.sharding import PartitionSpec as P

N = 96
RAD = 12
KG = 3840
NV = 16
PAIR = ("pair_0", "pair_1")
PAIR_GCOL = ("pair_0", "pair_1", "gcol")


def in_blocks(shard, dim, size):
    dims = shard.shape
    parts = shard.reshape(*dims[:dim], size, dims[dim] // size, *dims[dim + 1 :])
    return jnp.moveaxis(parts, dim, 0)


def sent_and_summed(shard, axis, dim):
    parts = in_blocks(shard, dim, lax.axis_size(axis))
    arrived = lax.all_to_all(parts, axis, split_axis=0, concat_axis=0, tiled=True)
    return arrived.astype(jnp.float32).sum(axis=0)


def sent_to_all(shard, axis):
    copies = jnp.broadcast_to(shard, (lax.axis_size(axis), *shard.shape))
    return lax.all_to_all(copies, axis, split_axis=0, concat_axis=0, tiled=True)


def in_order(parts, dim):
    parts = jnp.moveaxis(parts, 0, dim)
    dims = parts.shape
    return parts.reshape(*dims[:dim], dims[dim] * dims[dim + 1], *dims[dim + 2 :])


def collect(shard, axis, dim):
    parts = sent_to_all(shard, axis)
    return in_order(parts, dim)


def gathered_by_axis(shard, axes, dim):
    for axis in reversed(axes):
        shard = lax.all_gather(shard, axis, axis=dim, tiled=True)
    return shard


def wave_tables(positions, frequencies):
    phases = jnp.mod(positions[:, None] * frequencies[None, :], N).astype(jnp.float32) * (
        2.0 * math.pi / N
    )
    return (jnp.cos(phases), jnp.sin(phases))


def build_tables(x_positions):
    all_freq = jnp.arange(-RAD, RAD + 1, dtype=jnp.int32)
    pos_freq = jnp.arange(1, RAD + 1, dtype=jnp.int32)
    positions = jnp.arange(N, dtype=jnp.int32)
    cosine, sine_part = wave_tables(positions, all_freq)
    z_table = jnp.concatenate([cosine, sine_part], 1).astype(jnp.bfloat16)
    y_table = jnp.stack(
        [jnp.stack([cosine, sine_part], 1), jnp.stack([-sine_part, cosine], 1)], 1
    ).astype(jnp.bfloat16)
    x_cos, x_sin = wave_tables(x_positions, pos_freq)
    x_table = jnp.stack([jnp.stack([x_cos, -x_sin], 1), jnp.stack([-x_sin, -x_cos], 1)], 1).astype(
        jnp.bfloat16
    )
    return (z_table, y_table, x_table)


def pair_product(left_rows, right_rows):
    return lax.dot_general(
        left_rows, right_rows, (((0,), (0,)), ((), ())), preferred_element_type=jnp.float32
    )


def body(valence, conduction, val_energy, cond_energy, val_occupation, gvectors):
    pair_count = lax.axis_size(PAIR)
    gcol_count = lax.axis_size("gcol")
    planes = valence.shape[1]
    cond_bands = conduction.shape[0]
    extent = 2 * RAD + 1
    local_pairs = cond_bands * NV
    x_positions = lax.axis_index("grow") * planes + jnp.arange(planes, dtype=jnp.int32)
    z_table, y_table, x_table = build_tables(x_positions)
    flat_index = ((gvectors[0] - 1) * extent + gvectors[1] + RAD) * extent + gvectors[2] + RAD
    density = conduction[:, None] * valence[None]
    section_one = jnp.dot(
        density.reshape(-1, N), z_table, preferred_element_type=jnp.float32
    ).astype(jnp.bfloat16)
    section_one = section_one.reshape(local_pairs * planes, N, 2, extent)
    second = jnp.einsum(
        "ayik,yioj->aojk", section_one, y_table, preferred_element_type=jnp.float32
    ).astype(jnp.bfloat16)
    second = second.reshape(local_pairs, planes, 2, extent * extent)
    section_three = jnp.einsum(
        "pxoq,xosm->psmq", second, x_table, preferred_element_type=jnp.float32
    )
    section_three = section_three.reshape(local_pairs, 2, RAD * extent * extent)
    picked = jnp.take(section_three, flat_index, axis=2).reshape(local_pairs, 2 * KG)
    summed = sent_and_summed(picked.astype(jnp.bfloat16), "grow", 1)
    first_band = (lax.axis_index(PAIR) * gcol_count + lax.axis_index("gcol")) * cond_bands
    own_energy = lax.dynamic_slice_in_dim(cond_energy, first_band, cond_bands, 0)
    weight = val_occupation.astype(jnp.float32)[None, :] / (
        4.0 * (own_energy[:, None] - val_energy[None, :])
    )
    factor = (jnp.sqrt(weight) * (1.0 / N**1.5)).reshape(local_pairs, 1)
    weighted = (summed * factor).astype(jnp.bfloat16)
    prefactor = -1.0 / math.sqrt(pair_count * gcol_count * local_pairs)
    full_rows = collect(weighted, "grow", 1)
    row_part = lax.all_to_all(full_rows, PAIR, split_axis=1, concat_axis=0, tiled=True)
    partial_value = pair_product(row_part, gathered_by_axis(weighted, PAIR, 0))
    return sent_and_summed((partial_value * prefactor).astype(jnp.bfloat16), "gcol", 0)


def solution(mesh):
    finer = Mesh(
        mesh.devices.reshape(8, 4, mesh.shape["grow"], mesh.shape["gcol"]),
        ("pair_0", "pair_1", "grow", "gcol"),
    )
    placed = (P(None, "grow", None), P(PAIR_GCOL, "grow", None), P(), P(), P(), P())
    return jax.shard_map(
        body, mesh=finer, in_specs=placed, out_specs=P(PAIR_GCOL, "grow"), check_vma=False
    )
```

profile of v0, /device:TPU:2, one launch (start us, length us, event | category | flops | bytes accessed | tf_op | source)
XLA Modules:
  0.0 236.7 jit_solution(16631921713440293412)
XLA Ops:
  6.5 0.2 cosine_convert_fusion
  6.7 0.2 fusion.26
  6.9 6.3 %copy.37 = bf16[16,12,9216]{2,1,0:T(8,128)(2,1)} copy(bf16[16,12,9216]{2,0,1:T(8,128)(2,1)} %param.6) | data formatting | bytes 7077888 | tf_op args[0]
  13.3 6.8 %broadcast_multiply_fusion = bf16[2,16,12,9216]{3,2,1,0:T(8,128)(2,1)} fusion(bf16[16,12,9216]{2,1,0:T(8,128)(2,1)} %copy.37, bf16[2,12,9216]{2,1,0:T(8,128)(2,1)S(1)} %copy.36), kind=kLoop, calls=%fused_computation.4 | loop fusion | flops 3538944 | bytes 11059200 | tf_op jit(solution)/shard_map/mul | solution.py:90
  20.1 16.5 %mul.250 = bf16[36864,96]{1,0:T(8,128)(2,1)} reshape(bf16[2,16,12,9216]{3,2,1,0:T(8,128)(2,1)} %broadcast_multiply_fusion) | data formatting | bytes 14155776 | tf_op jit(solution)/shard_map/mul | solution.py:90
  36.6 11.3 %convolution_convert_fusion = bf16[36864,50]{0,1:T(8,128)(2,1)} fusion(bf16[36864,96]{1,0:T(8,128)(2,1)} %mul.250, bf16[96,25]{0,1:T(8,128)(2,1)S(1)} %get-tuple-element.19, bf16[96,25]{0,1:T(8,128)(2,1)S(1)} %get-tuple-element.18), kind=kOutput, calls=%fused_computation.1 | convolution fusion | flops 355756800 | bytes 10773888 | tf_op jit(solution)/shard_map/dot_general | solution.py:91
  47.9 8.5 %reshape.406 = bf16[384,96,2,25]{1,0,3,2:T(8,128)(2,1)} reshape(bf16[36864,50]{0,1:T(8,128)(2,1)} %convolution_convert_fusion) | data formatting | bytes 7372800 | tf_op jit(solution)/shard_map/reshape | solution.py:94
  56.4 4.0 %fusion.4 = bf16[384,2,25,25]{0,2,3,1:T(8,128)(2,1)S(1)} fusion(bf16[384,96,2,25]{1,0,3,2:T(8,128)(2,1)} %reshape.406, bf16[96,1,2,25]{0,3,1,2:T(8,128)(2,1)S(1)} %get-tuple-element.9, bf16[96,1,2,25]{0,3,1,2:T(8,128)(2,1)S(1)} %get-tuple-element.8), kind=kOutput, calls=%fused_computation.7 | convolution fusion | flops 184838400 | bytes 4665600 | tf_op jit(solution)/shard_map/ayik,yioj->aojk/dot_general | solution.py:95
  60.4 10.2 %copy.39 = bf16[384,2,25,25]{3,2,1,0:T(8,128)(2,1)} copy(bf16[384,2,25,25]{0,2,3,1:T(8,128)(2,1)S(1)} %fusion.4) | data formatting | bytes 1920000 | tf_op jit(solution)/shard_map/convert_element_type | solution.py:97
  70.6 12.4 %reshape.407 = bf16[32,12,2,625]{3,2,1,0:T(2,128)(2,1)S(1)} reshape(bf16[384,2,25,25]{3,2,1,0:T(8,128)(2,1)} %copy.39) | data formatting | bytes 1920000 | tf_op jit(solution)/shard_map/reshape | solution.py:98
  83.0 0.1 fusion.38
  83.2 0.6 convolution_bitcast_fusion
  83.7 5.8 %copy.53 = bf16[32,2,12,625]{0,1,3,2:T(2,128)(2,1)} copy(bf16[32,2,12,625]{3,2,0,1:T(8,128)(2,1)S(1)} %convolution_bitcast_fusion) | data formatting | bytes 1920000 | tf_op jit(solution)/shard_map/reshape | solution.py:102
  89.5 0.1 add_reduce_fusion.1
  89.7 12.5 %gather_fusion = bf16[3840,32,2]{1,2,0:T(2,128)(2,1)S(1)} fusion(bf16[32,2,7500]{0,1,2:T(2,128)(2,1)} %bitcast.66, s32[4096]{0:T(1024)S(1)} %pad_clamp_fusion), kind=kCustom, calls=%fused_computation | custom fusion | bytes 998400 | tf_op jit(solution)/shard_map/jit(_take)/gather | solution.py:103
  102.2 2.0 copy.42
  104.2 0.5 gather.7
  104.9 0.1 fusion.10
  105.0 1.1 copy.43
  106.1 7.3 %all-to-all-start = ((bf16[8,32,960]{2,1,0:T(8,128)(2,1)}), bf16[8,32,960]{2,1,0:T(8,128)(2,1)S(1)}, u32[]{:S(2)}, u32[]{:S(2)}) async-start(bf16[8,32,960]{2,1,0:T(8,128)(2,1)} %copy.43), calls=%async_computation | async-start | bytes 1048576 | tf_op jit(solution)/shard_map/all_to_all | solution.py:25
  113.6 0.1 reshape.415
  113.7 15.0 %all-to-all-done = bf16[8,32,960]{2,1,0:T(8,128)(2,1)S(1)} async-done(((bf16[8,32,960]{2,1,0:T(8,128)(2,1)}), bf16[8,32,960]{2,1,0:T(8,128)(2,1)S(1)}, u32[]{:S(2)}, u32[]{:S(2)}) %all-to-all-start) | async-done | bytes 491552 | tf_op jit(solution)/shard_map/all_to_all | solution.py:25
  128.9 15.4 %all_gather.6 = bf16[128,960]{1,0:T(8,128)(2,1)} all-gather(bf16[32,960]{1,0:T(8,128)(2,1)S(1)} %multiply_convert_fusion), channel_id=1, replica_groups=mesh['pair_0'=8,'pair_1'=4,'grow'=8,'gcol'=3] {'pair_1'}, dimensions={0}, use_global_device_ids=true | all-gather | bytes 307200 | tf_op jit(solution)/shard_map/all_gather | solution.py:47
  144.4 17.7 %all_to_all.34 = bf16[8,32,960]{2,1,0:T(8,128)(2,1)S(1)} all-to-all(bf16[8,32,960]{2,1,0:T(8,128)(2,1)S(1)} %broadcast_in_dim.30), channel_id=1, replica_groups=mesh['pair_0'=8,'pair_1'=4,'grow'=8,'gcol'=3] {'grow'}, dimensions={0} | all-to-all | bytes 983040 | tf_op jit(solution)/shard_map/all_to_all | solution.py:31
  162.1 0.3 copy.44
  162.4 0.6 all_to_all.25
  163.0 0.3 copy.45
  163.3 30.3 %all_to_all.35 = bf16[32,32,240]{2,0,1:T(8,128)(2,1)S(1)} all-to-all(bf16[32,32,240]{2,0,1:T(8,128)(2,1)S(1)} %copy.45), channel_id=1, replica_groups=mesh['pair_0'=8,'pair_1'=4,'grow'=8,'gcol'=3] {'pair_0','pair_1'}, dimensions={1} | all-to-all | bytes 983040 | tf_op jit(solution)/shard_map/all_to_all | solution.py:114
  193.6 5.9 %all-gather.2.cloned.1.call-done = bf16[1024,960]{1,0:T(8,128)(2,1)} async-done(((bf16[128,960]{1,0:T(8,128)(2,1)}), bf16[1024,960]{1,0:T(8,128)(2,1)}) %all-gather.2.cloned.1.call-update) | async-done | bytes 1966096 | tf_op jit(solution)/shard_map/all_gather | solution.py:47
  199.5 2.3 fusion.9
  201.8 27.3 %all_to_all.36 = bf16[3,80,960]{2,1,0:T(8,128)(2,1)S(1)} all-to-all(bf16[3,80,960]{2,1,0:T(8,128)(2,1)S(1)} %bitcast.68), channel_id=1, replica_groups=mesh['pair_0'=8,'pair_1'=4,'grow'=8,'gcol'=3] {'gcol'}, dimensions={0} | all-to-all | bytes 921600 | tf_op jit(solution)/shard_map/all_to_all | solution.py:25
  229.1 0.8 convert_reduce_fusion.1
  (30 shorter events, 0.8 us)
Async XLA Ops:
  6.9 6.3 %copy-start = (bf16[2,12,9216]{2,0,1:T(2,128)(2,1)S(1)}, bf16[2,12,9216]{2,0,1:T(2,128)(2,1)}, u32[]{:S(2)}) copy-start(bf16[2,12,9216]{2,0,1:T(2,128)(2,1)} %param.7) | copy-start | bytes 1327108
  83.0 6.5 %copy-start.1 = (s32[3,3840]{1,0:T(4,128)S(1)}, s32[3,3840]{1,0:T(4,128)}, u32[]{:S(2)}) copy-start(s32[3,3840]{1,0:T(4,128)} %param.11) | copy-start | bytes 138244
  89.5 23.9 %copy-start.4 = (s32[16]{0:T(128)S(1)}, s32[16]{0:T(128)}, u32[]{:S(2)}) copy-start(s32[16]{0:T(128)} %param.10) | copy-start | bytes 196
  89.5 24.0 %copy-start.3 = (f32[192]{0:T(256)S(1)}, f32[192]{0:T(256)}, u32[]{:S(2)}) copy-start(f32[192]{0:T(256)} %param.9) | copy-start | bytes 2308
  89.5 24.1 %copy-start.2 = (f32[16]{0:T(128)S(1)}, f32[16]{0:T(128)}, u32[]{:S(2)}) copy-start(f32[16]{0:T(128)} %param.8) | copy-start | bytes 196
  106.1 22.6 %all-to-all-start = ((bf16[8,32,960]{2,1,0:T(8,128)(2,1)}), bf16[8,32,960]{2,1,0:T(8,128)(2,1)S(1)}, u32[]{:S(2)}, u32[]{:S(2)}) async-start(bf16[8,32,960]{2,1,0:T(8,128)(2,1)} %copy.43), calls=%async_computation | async-start | bytes 1048576 | tf_op jit(solution)/shard_map/all_to_all | solution.py:25
  113.4 86.1 %all-gather.2.cloned.1.call-start = ((), (), s32[]{:S(2)}) async-start(), calls=%async_computation.4 | async-start | bytes 2359296 | tf_op jit(solution)/shard_map/all_gather | solution.py:47
Sparse Core Ops, SparseCore 0:
  144.4 55.0 all-gather.1
where the time goes:
time: 238 us; the launch traced here: 237 us
  blocking collectives  90.8 us (38%)
  local copies, waits for them, and re-layouts  77.3 us (32%)
  waiting for transfers between devices  20.9 us (9%)
  matrix products  18.1 us (8%)
  between operations  13.6 us (6%)
  other arithmetic  8.63 us (4%)
  starting transfers between devices  7.3 us (3%)
    all_to_all x1, blocking collectives, body(): lax.all_to_all(full_rows, PAIR, split_axis=1, concat_axis=0, tiled=True)  30.3 us
    all_to_all x1, blocking collectives, sent_and_summed(): lax.all_to_all(parts, axis, split_axis=0, concat_axis=0, tiled=True)  27.3 us
    all_to_all x1, blocking collectives, sent_to_all(): return lax.all_to_all(copies, axis, split_axis=0, concat_axis=0, tiled=True)  17.7 us
    mul x1, local copies, waits for them, and re-layouts, body(): density = conduction[:, None] * valence[None]  16.5 us
    all_gather x1, blocking collectives, gathered_by_axis(): shard = lax.all_gather(shard, axis, axis=dim, tiled=True)  15.4 us
    all_to_all x1, waiting for transfers between devices, sent_and_summed(): lax.all_to_all(parts, axis, split_axis=0, concat_axis=0, tiled=True)  15 us
    gather x3, local copies, waits for them, and re-layouts, body(): jnp.take(section_three, flat_index, axis=2).reshape(local_pairs, 2 * KG)  15 us
    reshape x1, local copies, waits for them, and re-layouts, body(): second = second.reshape(local_pairs, planes, 2, extent * extent)  12.4 us
  transfers between devices with their start and end apart: 2, of which 2 were waited for; matrix products, arithmetic and copies ran while one was open for 0% of the time, Pallas kernels for 0%

commit v1 on v0

v1 whole, which is shorter than its diff:
```python
import functools
import math

import jax
import jax.numpy as jnp
import numpy as np
from jax import lax
from jax.experimental import pallas as pl
from jax.experimental.pallas import tpu as pltpu
from jax.sharding import Mesh
from jax.sharding import PartitionSpec as P

PAIR = ("pair_0", "pair_1")
PAIR_GCOL = ("pair_0", "pair_1", "gcol")

N=96; RAD=12; KG=3840; NV=16
PL=12
PART=1152
HALF=math.sqrt(0.5)

def lane_waves():
    j=np.zeros((4,128),np.int64); k=np.zeros((4,128),np.int64); used=np.zeros((4,2,128))
    for l in range(91):
        j[0,l],k[0,l]=(-8+8*(l//13),l%13) if l<39 else (-12+8*((l-39)//13),(l-39)%13)
        used[0,0 if l<39 else 1,l]=1
    for c in (1,2,3):
        for l in range(75):
            j[c,l],k[c,l]=c-8+8*(l//25),l%25-12
            used[c,:,l]=1
    return j,k,used

def phase_of(n): return 2*np.pi*np.mod(n,N)/N

def tables():
    j,k,used=lane_waves()
    z=np.arange(N); y=np.arange(12)
    kz=phase_of(z[None,:,None]*k[:2,None,:])
    z_tab=np.stack([np.cos(kz),np.sin(kz)],1).astype(np.float32)
    jy=phase_of(y[None,:,None]*j[:,None,:])
    y_tab=np.stack([np.cos(jy),np.sin(jy)],1)
    first=np.where(used[:,0,None,None,:]>0,y_tab,0.0)
    y_tab0=np.where(used[0,1,None,None,:]>0,y_tab[0],0.0)
    y_all=np.concatenate([first,y_tab0[None]],0).astype(np.float32)
    a=np.arange(16)
    X=np.arange(N).reshape(8,12)
    ax=phase_of(X[:,:,None]*a[None,None,:])
    x_tab=np.zeros((8,32,16),np.float32)
    x_tab[:,:12]=np.cos(ax); x_tab[:,16:28]=np.sin(ax)
    return z_tab,y_all,x_tab

def transform_body(grow, val, con, gvec, z_tab, y_tab, x_tab, out, vbuf, cbuf, tab, mixed, sec_re, sec_im, keys, sems):
    copies=[]
    for s in range(4):
        copies.append((pltpu.make_async_copy(val.at[pl.ds(3*s,3)],vbuf.at[pl.ds(3*s,3)],sems.at[s]),
                       pltpu.make_async_copy(con.at[pl.ds(3*s,3)],cbuf.at[pl.ds(3*s,3)],sems.at[4+s])))
    for pair in copies:
        for c in pair: c.start()
    def build(yp,_):
        row=pl.ds(pl.multiple_of(yp*N,32),N)
        for t in range(4):
            cz=z_tab[min(t,1),0]; sz=z_tab[min(t,1),1]
            cy=y_tab[t,0,pl.ds(yp,1)]; sy=y_tab[t,1,pl.ds(yp,1)]
            co=(cy*cz-sy*sz); si=(sy*cz+cy*sz)
            tab[t,row,0:128]=co.astype(jnp.bfloat16)
            tab[t,row,128:256]=si.astype(jnp.bfloat16)
            row2=pl.ds(pl.multiple_of(PART+yp*N,32),N)
            if t==0:
                cy=y_tab[4,0,pl.ds(yp,1)]; sy=y_tab[4,1,pl.ds(yp,1)]
                tab[t,row2,0:128]=(cy*cz-sy*sz).astype(jnp.bfloat16)
                tab[t,row2,128:256]=(sy*cz+cy*sz).astype(jnp.bfloat16)
            else:
                tab[t,row2,0:128]=(-si).astype(jnp.bfloat16)
                tab[t,row2,128:256]=co.astype(jnp.bfloat16)
        return 0
    lax.fori_loop(0,12,build,0)
    for b in range(4):
        lanes=pl.ds(960*b,960)
        a=gvec[0:1,lanes]; j=gvec[1:2,lanes]; k=gvec[2:3,lanes]
        j8=j&7
        flip=(j8>=5)|(((j8&3)==0)&((k<0)|((k==0)&(j<0))))
        j=jnp.where(flip,-j,j); k=jnp.where(flip,-k,k)
        c=j&7
        odd=128*c+25*((j+8-c)>>3)+k+12
        even=jnp.where(c==0,13*((j+8)>>3)+k,39+13*((j+12)>>3)+k)
        rho=jnp.where((c&3)==0,even,odd)
        keys[b,0:1,0:960]=rho
        keys[b,1:2,0:960]=a
        keys[b,2:3,0:960]=flip.astype(jnp.int32)
    def mix(x,_):
        for c in range(2):
            row=pl.ds(pl.multiple_of(x*32+16*c,16),16)
            for w in range(0,PART,384):
                d=[]
                for q in range(8):
                    lanes=pl.ds(q*PART+w,384)
                    d.append((vbuf[x,:,lanes]*cbuf[x,c:c+1,lanes]).astype(jnp.float32))
                a=[d[q]+d[q+4] for q in range(4)]
                m=[d[q]-d[q+4] for q in range(4)]
                p=(m[1]-m[3])*HALF; r=(m[1]+m[3])*HALF
                even=a[0]+a[2]; odd=a[1]+a[3]
                for t,(u,v) in enumerate([(even+odd,even-odd),(m[0]+p,m[2]+r),(a[0]-a[2],a[1]-a[3]),(m[0]-p,r-m[2])]):
                    mixed[t,row,w:w+384]=u.astype(jnp.bfloat16)
                    mixed[t,row,PART+w:PART+w+384]=v.astype(jnp.bfloat16)
        return 0
    for s in range(4):
        for c in copies[s]: c.wait()
        lax.fori_loop(3*s,3*s+3,mix,0)
    for t in range(4):
        both=jnp.dot(mixed[t],tab[t],preferred_element_type=jnp.float32)
        sec_re[:,128*t:128*(t+1)]=both[:,:128].astype(jnp.bfloat16)
        sec_im[:,128*t:128*(t+1)]=both[:,128:].astype(jnp.bfloat16)
    waves=x_tab[grow]
    def pick(b,_):
        for n0 in range(0,960,256):
            w=min(256,960-n0)
            lanes=pl.ds(n0,w)
            rho=keys[b,0:1,lanes]; a=keys[b,1:2,lanes]; sign=1.0-2.0*keys[b,2:3,lanes].astype(jnp.float32)
            hot=(lax.broadcasted_iota(jnp.int32,(512,w),0)==rho).astype(jnp.float32).astype(jnp.bfloat16)
            hot_a=(lax.broadcasted_iota(jnp.int32,(16,w),0)==a).astype(jnp.float32).astype(jnp.bfloat16)
            wave=jnp.dot(waves,hot_a,preferred_element_type=jnp.float32)
            re=jnp.dot(sec_re[...],hot,preferred_element_type=jnp.float32)
            im=jnp.dot(sec_im[...],hot,preferred_element_type=jnp.float32)
            tot_re=jnp.zeros((32,w),jnp.float32); tot_im=jnp.zeros((32,w),jnp.float32)
            for x in range(PL):
                co=wave[x:x+1]; si=wave[16+x:17+x]
                gr=re[32*x:32*x+32]; gi=im[32*x:32*x+32]
                tot_re+=co*gr-(si*sign)*gi
                tot_im+=si*gr+(co*sign)*gi
            out[b,:,lanes]=tot_re.astype(out.dtype)
            out[4+b,:,lanes]=(-tot_im).astype(out.dtype)
        return 0
    lax.fori_loop(0,4,pick,0)

def transform_scratch():
    return [pltpu.VMEM((PL,NV,9216),jnp.bfloat16), pltpu.VMEM((PL,2,9216),jnp.bfloat16),
        pltpu.VMEM((4,2*PART,256),jnp.bfloat16), pltpu.VMEM((4,384,2*PART),jnp.bfloat16),
        pltpu.VMEM((384,512),jnp.bfloat16), pltpu.VMEM((384,512),jnp.bfloat16),
        pltpu.VMEM((4,8,1024),jnp.int32), pltpu.SemaphoreType.DMA((8,))]


def kernel(*refs):
    transform_body(lax.axis_index("grow"), *refs)

def partial_sums(valence, conduction, gvectors):
    z_tab, y_tab, x_tab = tables()
    return pl.pallas_call(
        kernel,
        out_shape=jax.ShapeDtypeStruct((8, 32, 960), jnp.bfloat16),
        in_specs=[pl.BlockSpec(memory_space=pl.ANY)] * 2
        + [pl.BlockSpec(memory_space=pltpu.VMEM)] * 4,
        out_specs=pl.BlockSpec(memory_space=pltpu.VMEM),
        scratch_shapes=transform_scratch(),
        compiler_params=pltpu.CompilerParams(vmem_limit_bytes=48 * 2**20),
        name="transform",
    )(valence.transpose(1, 0, 2), conduction.transpose(1, 0, 2), gvectors,
      jnp.asarray(z_tab), jnp.asarray(y_tab), jnp.asarray(x_tab, jnp.bfloat16))

def in_blocks(shard, dim, size):
    dims = shard.shape
    parts = shard.reshape(*dims[:dim], size, dims[dim] // size, *dims[dim + 1 :])
    return jnp.moveaxis(parts, dim, 0)


def sent_and_summed(shard, axis, dim):
    parts = in_blocks(shard, dim, lax.axis_size(axis))
    arrived = lax.all_to_all(parts, axis, split_axis=0, concat_axis=0, tiled=True)
    return arrived.astype(jnp.float32).sum(axis=0)


def sent_to_all(shard, axis):
    copies = jnp.broadcast_to(shard, (lax.axis_size(axis), *shard.shape))
    return lax.all_to_all(copies, axis, split_axis=0, concat_axis=0, tiled=True)


def in_order(parts, dim):
    parts = jnp.moveaxis(parts, 0, dim)
    dims = parts.shape
    return parts.reshape(*dims[:dim], dims[dim] * dims[dim + 1], *dims[dim + 2 :])


def collect(shard, axis, dim):
    parts = sent_to_all(shard, axis)
    return in_order(parts, dim)


def gathered_by_axis(shard, axes, dim):
    for axis in reversed(axes):
        shard = lax.all_gather(shard, axis, axis=dim, tiled=True)
    return shard


def pair_product(left_rows, right_rows):
    return lax.dot_general(
        left_rows, right_rows, (((0,), (0,)), ((), ())), preferred_element_type=jnp.float32
    )


def body(valence, conduction, val_energy, cond_energy, val_occupation, gvectors):
    pair_count = lax.axis_size(PAIR)
    gcol_count = lax.axis_size("gcol")
    cond_bands = conduction.shape[0]
    local_pairs = cond_bands * NV
    parts = partial_sums(valence, conduction, gvectors)
    arrived = lax.all_to_all(parts, "grow", split_axis=0, concat_axis=0, tiled=True)
    summed = arrived.astype(jnp.float32).sum(axis=0)
    first_band = (lax.axis_index(PAIR) * gcol_count + lax.axis_index("gcol")) * cond_bands
    own_energy = lax.dynamic_slice_in_dim(cond_energy, first_band, cond_bands, 0)
    weight = val_occupation.astype(jnp.float32)[None, :] / (
        4.0 * (own_energy[:, None] - val_energy[None, :])
    )
    factor = (jnp.sqrt(weight) * (1.0 / N**1.5)).reshape(local_pairs, 1)
    weighted = (summed * factor).astype(jnp.bfloat16)
    prefactor = -1.0 / math.sqrt(pair_count * gcol_count * local_pairs)
    full_rows = collect(weighted, "grow", 1)
    row_part = lax.all_to_all(full_rows, PAIR, split_axis=1, concat_axis=0, tiled=True)
    partial_value = pair_product(row_part, gathered_by_axis(weighted, PAIR, 0))
    return sent_and_summed((partial_value * prefactor).astype(jnp.bfloat16), "gcol", 0)


def solution(mesh):
    finer = Mesh(
        mesh.devices.reshape(8, 4, mesh.shape["grow"], mesh.shape["gcol"]),
        ("pair_0", "pair_1", "grow", "gcol"),
    )
    placed = (P(None, "grow", None), P(PAIR_GCOL, "grow", None), P(), P(), P(), P())
    return jax.shard_map(
        body, mesh=finer, in_specs=placed, out_specs=P(PAIR_GCOL, "grow"), check_vma=False
    )
```

time: 238 us -> 158 us (0.66)
  the two profiles are of different devices: /device:TPU:2 before, /device:TPU:4 now
where the time goes in v1:
time: 158 us
  blocking collectives  90.7 us (57%)
  waiting for transfers between devices  21.1 us (13%)
  Pallas kernels  14.1 us (9%)
  between operations  13.5 us (9%)
  local copies, waits for them, and re-layouts  7.86 us (5%)
  starting transfers between devices  7.31 us (5%)
  matrix products  2.28 us (1%)
    all_to_all x1, blocking collectives, body(): lax.all_to_all(full_rows, PAIR, split_axis=1, concat_axis=0, tiled=True)  28.9 us
    all_to_all x1, blocking collectives, sent_and_summed(): lax.all_to_all(parts, axis, split_axis=0, concat_axis=0, tiled=True)  27.2 us
    all_to_all x1, blocking collectives, sent_to_all(): return lax.all_to_all(copies, axis, split_axis=0, concat_axis=0, tiled=True)  17.7 us
    all_gather x1, blocking collectives, gathered_by_axis(): shard = lax.all_gather(shard, axis, axis=dim, tiled=True)  16.9 us
    all_to_all x1, waiting for transfers between devices, body(): lax.all_to_all(parts, 'grow', split_axis=0, concat_axis=0, tiled=True)  15 us
    pallas_call x1, Pallas kernels, partial_sums(): pl.pallas_call(kernel, out_shape=jax.ShapeDtypeStruct((8, 32, 960), jnp.b...  14.1 us
    all_to_all x1, starting transfers between devices, body(): lax.all_to_all(parts, 'grow', split_axis=0, concat_axis=0, tiled=True)  7.27 us
    unnamed x18, local copies, waits for them, and re-layouts  6.5 us
  transfers between devices with their start and end apart: 2, of which 2 were waited for; matrix products, arithmetic and copies ran while one was open for 1% of the time, Pallas kernels for 0%

profile of v1, /device:TPU:4, one launch (start us, length us, event | category | flops | bytes accessed | tf_op | source)
XLA Modules:
  0.0 157.8 jit_solution(17634825093476064488)
XLA Ops:
  6.5 0.0 copy-start
  6.5 2.0 %copy-done = bf16[16,12,9216]{2,0,1:T(8,128)(2,1)S(1)} copy-done((bf16[16,12,9216]{2,0,1:T(8,128)(2,1)S(1)}, bf16[16,12,9216]{2,0,1:T(8,128)(2,1)}, u32[]{:S(2)}) %copy-start) | copy-done | bytes 3538968
  8.5 0.0 copy-start.1
  8.5 1.0 copy-done.1
  9.6 0.9 copy-done.2
  10.5 0.9 copy-done.3
  11.4 0.8 copy-done.4
  12.2 0.8 copy-done.5
  13.0 14.1 %transform.1 = bf16[8,32,960]{2,1,0:T(8,128)(2,1)} custom-call(bf16[12,16,9216]{2,1,0:T(8,128)(2,1)S(1)} %bitcast.9, bf16[12,2,9216]{2,1,0:T(2,128)(2,1)S(1)} %bitcast.10, s32[3,3840]{1,0:T(4,128)S(1)} %copy-done.5, f32[2,2,96,128]{3,2,1,0:T(8,128)S(1)} %copy-done.2, f32[5,2,12,128]{3,2,1,0:T(8,128)S(1)} %copy-done.3, bf16[8,32,16]{2,1,0:T(8,128)(2,1)S(1)} %copy-done.4), custom_call_target="tpu_custom_call" | custom-call | tf_op jit(solution)/shard_map/transform/pallas_call | solution.py:146
  27.1 7.3 %all-to-all-start = ((bf16[8,32,960]{2,1,0:T(8,128)(2,1)}), bf16[8,32,960]{2,1,0:T(8,128)(2,1)S(1)}, u32[]{:S(2)}, u32[]{:S(2)}) async-start(bf16[8,32,960]{2,1,0:T(8,128)(2,1)} %transform.1), calls=%async_computation | async-start | bytes 1048576 | tf_op jit(solution)/shard_map/all_to_all | solution.py:204
  34.4 0.0 all-gather.2.cloned.1.call-start
  34.5 0.0 copy-done.8
  34.5 0.0 copy-done.7
  34.5 0.1 dynamic_slice.3
  34.6 0.0 copy-done.6
  34.6 0.1 sqrt_multiply_fusion
  34.6 0.1 reshape.42
  34.7 15.0 %all-to-all-done = bf16[8,32,960]{2,1,0:T(8,128)(2,1)S(1)} async-done(((bf16[8,32,960]{2,1,0:T(8,128)(2,1)}), bf16[8,32,960]{2,1,0:T(8,128)(2,1)S(1)}, u32[]{:S(2)}, u32[]{:S(2)}) %all-to-all-start) | async-done | bytes 491552 | tf_op jit(solution)/shard_map/all_to_all | solution.py:204
  49.7 0.1 convert_reduce_fusion
  49.8 0.1 multiply_convert_fusion
  49.9 16.9 %all_gather.6 = bf16[128,960]{1,0:T(8,128)(2,1)} all-gather(bf16[32,960]{1,0:T(8,128)(2,1)S(1)} %multiply_convert_fusion), channel_id=1, replica_groups=mesh['pair_0'=8,'pair_1'=4,'grow'=8,'gcol'=3] {'pair_1'}, dimensions={0}, use_global_device_ids=true | all-gather | bytes 307200 | tf_op jit(solution)/shard_map/all_gather | solution.py:188
  66.7 0.0 all-gather.2.cloned.1.call-update
  66.8 0.1 broadcast_in_dim.2
  66.8 17.7 %all_to_all.34 = bf16[8,32,960]{2,1,0:T(8,128)(2,1)S(1)} all-to-all(bf16[8,32,960]{2,1,0:T(8,128)(2,1)S(1)} %broadcast_in_dim.2), channel_id=1, replica_groups=mesh['pair_0'=8,'pair_1'=4,'grow'=8,'gcol'=3] {'grow'}, dimensions={0} | all-to-all | bytes 983040 | tf_op jit(solution)/shard_map/all_to_all | solution.py:172
  84.6 0.3 copy.11
  84.9 0.6 all_to_all.25
  85.4 0.3 copy.12
  85.7 28.9 %all_to_all.35 = bf16[32,32,240]{2,0,1:T(8,128)(2,1)S(1)} all-to-all(bf16[32,32,240]{2,0,1:T(8,128)(2,1)S(1)} %copy.12), channel_id=1, replica_groups=mesh['pair_0'=8,'pair_1'=4,'grow'=8,'gcol'=3] {'pair_0','pair_1'}, dimensions={1} | all-to-all | bytes 983040 | tf_op jit(solution)/shard_map/all_to_all | solution.py:215
  114.6 6.1 %all-gather.2.cloned.1.call-done = bf16[1024,960]{1,0:T(8,128)(2,1)} async-done(((bf16[128,960]{1,0:T(8,128)(2,1)}), bf16[1024,960]{1,0:T(8,128)(2,1)}) %all-gather.2.cloned.1.call-update) | async-done | bytes 1966096 | tf_op jit(solution)/shard_map/all_gather | solution.py:188
  120.7 2.3 %fusion = bf16[240,960]{1,0:T(8,128)(2,1)S(1)} fusion(bf16[1024,240]{1,0:T(8,128)(2,1)S(1)} %bitcast.13, bf16[1024,960]{1,0:T(8,128)(2,1)} %all-gather.2.cloned.1.call-done), kind=kOutput, calls=%fused_computation.1 | convolution fusion | flops 472320000 | bytes 2918400 | tf_op jit(solution)/shard_map/dot_general | solution.py:193
  122.9 27.2 %all_to_all.36 = bf16[3,80,960]{2,1,0:T(8,128)(2,1)S(1)} all-to-all(bf16[3,80,960]{2,1,0:T(8,128)(2,1)S(1)} %bitcast.11), channel_id=1, replica_groups=mesh['pair_0'=8,'pair_1'=4,'grow'=8,'gcol'=3] {'gcol'}, dimensions={0} | all-to-all | bytes 921600 | tf_op jit(solution)/shard_map/all_to_all | solution.py:166
  150.2 0.8 convert_reduce_fusion.1
  (8 shorter events, 0.0 us)
Async XLA Ops:
  6.5 2.0 %copy-start = (bf16[16,12,9216]{2,0,1:T(8,128)(2,1)S(1)}, bf16[16,12,9216]{2,0,1:T(8,128)(2,1)}, u32[]{:S(2)}) copy-start(bf16[16,12,9216]{2,0,1:T(8,128)(2,1)} %param.9) | copy-start | bytes 10616836
  8.5 1.0 copy-start.1
  9.6 0.9 copy-start.2
  10.5 0.9 copy-start.3
  11.4 0.8 copy-start.4
  12.2 0.8 copy-start.5
  13.0 21.4 %copy-start.8 = (s32[16]{0:T(128)S(1)}, s32[16]{0:T(128)}, u32[]{:S(2)}) copy-start(s32[16]{0:T(128)} %param.13) | copy-start | bytes 196
  13.0 21.4 %copy-start.7 = (f32[192]{0:T(256)S(1)}, f32[192]{0:T(256)}, u32[]{:S(2)}) copy-start(f32[192]{0:T(256)} %param.12) | copy-start | bytes 2308
  13.0 21.5 %copy-start.6 = (f32[16]{0:T(128)S(1)}, f32[16]{0:T(128)}, u32[]{:S(2)}) copy-start(f32[16]{0:T(128)} %param.11) | copy-start | bytes 196
  27.1 22.6 %all-to-all-start = ((bf16[8,32,960]{2,1,0:T(8,128)(2,1)}), bf16[8,32,960]{2,1,0:T(8,128)(2,1)S(1)}, u32[]{:S(2)}, u32[]{:S(2)}) async-start(bf16[8,32,960]{2,1,0:T(8,128)(2,1)} %transform.1), calls=%async_computation | async-start | bytes 1048576 | tf_op jit(solution)/shard_map/all_to_all | solution.py:204
  34.4 86.3 %all-gather.2.cloned.1.call-start = ((), (), s32[]{:S(2)}) async-start(), calls=%async_computation.4 | async-start | bytes 2359296 | tf_op jit(solution)/shard_map/all_gather | solution.py:188
Sparse Core Ops, SparseCore 0:
  66.9 53.7 all-gather.1

commit v2 on v1

v2 whole, which is shorter than its diff:
```python
import functools
import math

import jax
import jax.numpy as jnp
import numpy as np
from jax import lax
from jax.experimental import pallas as pl
from jax.experimental.pallas import tpu as pltpu
from jax.sharding import Mesh
from jax.sharding import PartitionSpec as P

N=96; RAD=12; KG=3840; NV=16
PL=12
PART=1152
HALF=math.sqrt(0.5)

def lane_waves():
    j=np.zeros((4,128),np.int64); k=np.zeros((4,128),np.int64); used=np.zeros((4,2,128))
    for l in range(91):
        j[0,l],k[0,l]=(-8+8*(l//13),l%13) if l<39 else (-12+8*((l-39)//13),(l-39)%13)
        used[0,0 if l<39 else 1,l]=1
    for c in (1,2,3):
        for l in range(75):
            j[c,l],k[c,l]=c-8+8*(l//25),l%25-12
            used[c,:,l]=1
    return j,k,used

def phase_of(n): return 2*np.pi*np.mod(n,N)/N

def tables():
    j,k,used=lane_waves()
    z=np.arange(N); y=np.arange(12)
    kz=phase_of(z[None,:,None]*k[:2,None,:])
    z_tab=np.stack([np.cos(kz),np.sin(kz)],1).astype(np.float32)
    jy=phase_of(y[None,:,None]*j[:,None,:])
    y_tab=np.stack([np.cos(jy),np.sin(jy)],1)
    first=np.where(used[:,0,None,None,:]>0,y_tab,0.0)
    y_tab0=np.where(used[0,1,None,None,:]>0,y_tab[0],0.0)
    y_all=np.concatenate([first,y_tab0[None]],0).astype(np.float32)
    a=np.arange(16)
    X=np.arange(N).reshape(8,12)
    ax=phase_of(X[:,:,None]*a[None,None,:])
    x_tab=np.zeros((8,32,16),np.float32)
    x_tab[:,:12]=np.cos(ax); x_tab[:,16:28]=np.sin(ax)
    return z_tab,y_all,x_tab

def transform_body(val, con, gvec_in, z_in, y_in, x_in, out, vbuf, cbuf, gvec, z_tab, y_tab, x_tab, tab, mixed, sec_re, sec_im, keys, sems):
    grow=2*lax.axis_index("zl")+lax.axis_index("core")
    small=[pltpu.make_async_copy(a,b,sems.at[8+i]) for i,(a,b) in enumerate([(z_in,z_tab),(y_in,y_tab),(gvec_in,gvec),(x_in.at[grow],x_tab)])]
    for c in small: c.start()
    copies=[]
    for s in range(4):
        copies.append((pltpu.make_async_copy(val.at[pl.ds(3*s,3)],vbuf.at[pl.ds(3*s,3)],sems.at[s]),
                       pltpu.make_async_copy(con.at[pl.ds(3*s,3)],cbuf.at[pl.ds(3*s,3)],sems.at[4+s])))
    for pair in copies:
        for c in pair: c.start()
    for c in small: c.wait()
    def build(yp,_):
        row=pl.ds(pl.multiple_of(yp*N,32),N)
        for t in range(4):
            cz=z_tab[min(t,1),0]; sz=z_tab[min(t,1),1]
            cy=y_tab[t,0,pl.ds(yp,1)]; sy=y_tab[t,1,pl.ds(yp,1)]
            co=(cy*cz-sy*sz); si=(sy*cz+cy*sz)
            tab[t,row,0:128]=co.astype(jnp.bfloat16)
            tab[t,row,128:256]=si.astype(jnp.bfloat16)
            row2=pl.ds(pl.multiple_of(PART+yp*N,32),N)
            if t==0:
                cy=y_tab[4,0,pl.ds(yp,1)]; sy=y_tab[4,1,pl.ds(yp,1)]
                tab[t,row2,0:128]=(cy*cz-sy*sz).astype(jnp.bfloat16)
                tab[t,row2,128:256]=(sy*cz+cy*sz).astype(jnp.bfloat16)
            else:
                tab[t,row2,0:128]=(-si).astype(jnp.bfloat16)
                tab[t,row2,128:256]=co.astype(jnp.bfloat16)
        return 0
    lax.fori_loop(0,12,build,0)
    keys[...] = jnp.zeros_like(keys)
    for b in range(16):
        lanes=pl.ds(240*b,240)
        a=gvec[0:1,lanes]; j=gvec[1:2,lanes]; k=gvec[2:3,lanes]
        j8=j&7
        flip=(j8>=5)|(((j8&3)==0)&((k<0)|((k==0)&(j<0))))
        j=jnp.where(flip,-j,j); k=jnp.where(flip,-k,k)
        c=j&7
        odd=128*c+25*((j+8-c)>>3)+k+12
        even=jnp.where(c==0,13*((j+8)>>3)+k,39+13*((j+12)>>3)+k)
        lanes=pl.ds(256*(b%4),240)
        keys[b//4,0:1,lanes]=jnp.where((c&3)==0,even,odd)
        keys[b//4,1:2,lanes]=a
        keys[b//4,2:3,lanes]=flip.astype(jnp.int32)
    def mix(x,_):
        for c in range(2):
            row=pl.ds(pl.multiple_of(x*32+16*c,16),16)
            for w in range(0,PART,384):
                d=[]
                for q in range(8):
                    lanes=pl.ds(q*PART+w,384)
                    d.append((vbuf[x,:,lanes]*cbuf[x,c:c+1,lanes]).astype(jnp.float32))
                a=[d[q]+d[q+4] for q in range(4)]
                m=[d[q]-d[q+4] for q in range(4)]
                p=(m[1]-m[3])*HALF; r=(m[1]+m[3])*HALF
                even=a[0]+a[2]; odd=a[1]+a[3]
                for t,(u,v) in enumerate([(even+odd,even-odd),(m[0]+p,m[2]+r),(a[0]-a[2],a[1]-a[3]),(m[0]-p,r-m[2])]):
                    mixed[t,row,w:w+384]=u.astype(jnp.bfloat16)
                    mixed[t,row,PART+w:PART+w+384]=v.astype(jnp.bfloat16)
        return 0
    for s in range(4):
        for c in copies[s]: c.wait()
        lax.fori_loop(3*s,3*s+3,mix,0)
    for t in range(4):
        both=jnp.dot(mixed[t],tab[t],preferred_element_type=jnp.float32)
        sec_re[:,128*t:128*(t+1)]=both[:,:128].astype(jnp.bfloat16)
        sec_im[:,128*t:128*(t+1)]=both[:,128:].astype(jnp.bfloat16)
    waves=x_tab[...]
    def pick(b,_):
        for n0 in range(0,1024,256):
            w=256
            lanes=pl.ds(n0,w)
            rho=keys[b,0:1,lanes]; a=keys[b,1:2,lanes]; sign=1.0-2.0*keys[b,2:3,lanes].astype(jnp.float32)
            hot=(lax.broadcasted_iota(jnp.int32,(512,w),0)==rho).astype(jnp.float32).astype(jnp.bfloat16)
            hot_a=(lax.broadcasted_iota(jnp.int32,(16,w),0)==a).astype(jnp.float32).astype(jnp.bfloat16)
            wave=jnp.dot(waves,hot_a,preferred_element_type=jnp.float32)
            re=jnp.dot(sec_re[...],hot,preferred_element_type=jnp.float32)
            im=jnp.dot(sec_im[...],hot,preferred_element_type=jnp.float32)
            tot_re=jnp.zeros((32,w),jnp.float32); tot_im=jnp.zeros((32,w),jnp.float32)
            for x in range(PL):
                co=wave[x:x+1]; si=wave[16+x:17+x]
                gr=re[32*x:32*x+32]; gi=im[32*x:32*x+32]
                tot_re+=co*gr-(si*sign)*gi
                tot_im+=si*gr+(co*sign)*gi
            out[b//2,lax.rem(b,2),:,lanes]=tot_re.astype(out.dtype)
            out[2+b//2,lax.rem(b,2),:,lanes]=(-tot_im).astype(out.dtype)
        return 0
    lax.fori_loop(0,4,pick,0)

def transform_scratch():
    return [pltpu.VMEM((PL,NV,9216),jnp.bfloat16), pltpu.VMEM((PL,2,9216),jnp.bfloat16),
        pltpu.VMEM((3,KG),jnp.int32), pltpu.VMEM((2,2,96,128),jnp.float32), pltpu.VMEM((5,2,12,128),jnp.float32), pltpu.VMEM((32,16),jnp.bfloat16),
        pltpu.VMEM((4,2*PART,256),jnp.bfloat16), pltpu.VMEM((4,384,2*PART),jnp.bfloat16),
        pltpu.VMEM((384,512),jnp.bfloat16), pltpu.VMEM((384,512),jnp.bfloat16),
        pltpu.VMEM((4,8,1024),jnp.int32), pltpu.SemaphoreType.DMA((12,))]


def partial_sums(valence, conduction, gvectors):
    z_tab, y_tab, x_tab = tables()
    return pl.pallas_call(
        transform_body,
        out_shape=jax.ShapeDtypeStruct((4, 2, 32, 1024), jnp.bfloat16),
        in_specs=[pl.BlockSpec(memory_space=pl.ANY)] * 6,
        out_specs=pl.BlockSpec(memory_space=pltpu.VMEM),
        scratch_shapes=transform_scratch(),
        compiler_params=pltpu.CompilerParams(vmem_limit_bytes=48 * 2**20),
        name="transform",
    )(valence.transpose(1, 0, 2), conduction.transpose(1, 0, 2), gvectors,
      jnp.asarray(z_tab), jnp.asarray(y_tab), jnp.asarray(x_tab, jnp.bfloat16))

MESH_AXES = ("y", "x", "zl", "core", "zh")
SIDE = pl.DeviceIdType.MESH
SUB = 256
WIDE = 4 * SUB


def turned(axis, step):
    size = lax.axis_size(axis)
    return lax.rem(lax.axis_index(axis) + step % size, size)


def remote(src, dst, send_sem, recv_sem, target):
    return pltpu.make_async_remote_copy(src_ref=src, dst_ref=dst, send_sem=send_sem, recv_sem=recv_sem,
                                        device_id=target, device_id_type=SIDE)


def pair_factor(val_energy, cond_energy, occupation):
    first = ((lax.axis_index("y") * 4 + lax.axis_index("x")) * 3 + lax.axis_index("zh")) * 2
    row = lax.broadcasted_iota(jnp.int32, (32, 16), 0)
    at_v = lax.broadcasted_iota(jnp.int32, (32, 16), 1) == (row & 15)
    ev = jnp.sum(jnp.where(at_v, val_energy, 0.0), axis=1, keepdims=True)
    occ = jnp.sum(jnp.where(at_v, occupation.astype(jnp.float32), 0.0), axis=1, keepdims=True)
    row = lax.broadcasted_iota(jnp.int32, (32, 192), 0)
    at_c = lax.broadcasted_iota(jnp.int32, (32, 192), 1) == first + (row >> 4)
    ec = jnp.sum(jnp.where(at_c, cond_energy, 0.0), axis=1, keepdims=True)
    return jnp.sqrt(occ / (4.0 * (ec - ev))) * (1.0 / N**1.5)


def exchange_body(parts, val_energy, cond_energy, occupation, out,
                  core_in, z_out, z_in, cols, rows, x_out, x_in,
                  core_sems, z_sems, zh_sems, y_sems, row_sems, row_out_sems, x_sems):
    y, x, zl, core, zh = (lax.axis_index(a) for a in MESH_AXES)
    barrier = pltpu.get_barrier_semaphore()
    partners = ([{"core": 1 - core}] + [{"zl": turned("zl", k)} for k in (1, 2, 3)]
                + [{"zh": turned("zh", k)} for k in (1, 2)] + [{"y": turned("y", k)} for k in (1, 7)]
                + [{"x": turned("x", k)} for k in (1, 2, 3)])
    for target in partners:
        pl.semaphore_signal(barrier, inc=1, device_id=target, device_id_type=SIDE)
    pl.semaphore_wait(barrier, len(partners))

    other = {"core": 1 - core}
    swaps = []
    for k in (2, 1, 3, 0):
        z = turned("zl", k)
        swaps.append((k, z, remote(parts.at[z, 1 - core], core_in.at[k], core_sems.at[0, k], core_sems.at[1, k], other)))
    for _, _, c in swaps:
        c.start()
    z_copies = []
    for k, z, c in swaps:
        c.wait_recv()
        both = parts[z, core].astype(jnp.float32) + core_in[k].astype(jnp.float32)
        if k:
            z_out[k - 1] = both.astype(jnp.bfloat16)
            c2 = remote(z_out.at[k - 1], z_in.at[k - 1], z_sems.at[0, k - 1], z_sems.at[1, k - 1], {"zl": z})
            c2.start()
            z_copies.append(c2)
        else:
            total = both
    factor = pair_factor(val_energy[...], cond_energy[...], occupation[...])
    for c in z_copies:
        c.wait_recv()
    for k in range(3):
        total = total + z_in[k].astype(jnp.float32)
    mine = zh * 8 + y
    cols[mine] = (total * factor).astype(jnp.bfloat16)

    zh_copies = []
    for k in (1, 2):
        c = remote(cols.at[mine], cols.at[mine], zh_sems.at[0, k - 1], zh_sems.at[1, k - 1], {"zh": turned("zh", k)})
        c.start()
        zh_copies.append(c)

    plane = 2 * zl + core
    home = y // 2
    on_chain = core == lax.rem(y, 2)
    source = plane == y

    def slot(t, step):
        return turned("zh", -t) * 8 + turned("y", step)

    def pick_rows(s):
        here = lax.broadcasted_iota(jnp.int32, (SUB, 128), 0)
        there = lax.broadcasted_iota(jnp.int32, (SUB, 128), 1)
        pick = ((here == there + 80 * zh) & (there < 80)).astype(jnp.float32).astype(jnp.bfloat16)
        for q in range(4):
            cut = jnp.dot(cols[s, :, SUB * q : SUB * (q + 1)], pick, preferred_element_type=jnp.float32)
            rows[s, :, 128 * q : 128 * (q + 1)] = cut.astype(jnp.bfloat16)

    def pass_rows(t, step):
        n = t * 8 + step % 8
        s = slot(t, step)

        def send(i, target):
            remote(rows.at[s], rows.at[s], row_out_sems.at[n, i], row_sems.at[n], target).start()

        @pl.when(source)
        def _():
            pick_rows(s)

        @pl.when(jnp.logical_not(source))
        def _():
            remote(rows.at[s], rows.at[s], row_out_sems.at[n, 0], row_sems.at[n], other).wait_recv()

        @pl.when(on_chain)
        def _():
            send(0, other)

        @pl.when(on_chain & (zl >= home) & (zl < 3))
        def _():
            send(1, {"zl": lax.rem(zl + 1, 4)})

        @pl.when(on_chain & (zl <= home) & (zl > 0))
        def _():
            send(2, {"zl": lax.rem(zl + 3, 4)})

    def ring(t, way, hop):
        s = slot(t, -way * (hop - 1))
        d = 0 if way == 1 else 1
        n = (t * 4 + hop - 1) * 2 + d
        half = pl.ds(0, 32) if hop < 4 else pl.ds(16 * d, 16)
        return remote(cols.at[s, half], cols.at[s, half], y_sems.at[0, n], y_sems.at[1, n], {"y": turned("y", way)})

    def landed(t, way, hop):
        s = slot(t, -way * hop)
        d = 0 if way == 1 else 1
        n = (t * 4 + hop - 1) * 2 + d
        half = pl.ds(0, 32) if hop < 4 else pl.ds(16 * d, 16)
        remote(cols.at[s, half], cols.at[s, half], y_sems.at[0, n], y_sems.at[1, n], {"y": turned("y", way)}).wait_recv()

    def start(t, hop):
        ring(t, 1, hop).start()
        ring(t, -1, hop).start()

    start(0, 1)
    pass_rows(0, 0)
    for hop in (1, 2, 3):
        landed(0, 1, hop)
        ring(0, 1, hop + 1).start()
        landed(0, -1, hop)
        ring(0, -1, hop + 1).start()
        pass_rows(0, -hop)
        pass_rows(0, hop)
    for t in (1, 2):
        zh_copies[t - 1].wait_recv()
        start(t, 1)
    for t in (1, 2):
        pass_rows(t, 0)
    landed(0, 1, 4)
    landed(0, -1, 4)
    pass_rows(0, 4)
    for hop in (1, 2, 3):
        for t in (1, 2):
            landed(t, 1, hop)
            ring(t, 1, hop + 1).start()
            landed(t, -1, hop)
            ring(t, -1, hop + 1).start()
        for t in (1, 2):
            pass_rows(t, -hop)
            pass_rows(t, hop)
    for t in (1, 2):
        landed(t, 1, 4)
        landed(t, -1, 4)
        pass_rows(t, 4)

    right = cols[...].reshape(768, WIDE)
    x_copies = []
    for k in (2, 1, 3, 0):
        q = turned("x", k)
        left = rows[:, :, pl.ds(pl.multiple_of(128 * q, 128), 128)].reshape(768, 128)
        block = lax.dot_general(left, right, (((0,), (0,)), ((), ())), preferred_element_type=jnp.float32)
        if k:
            x_out[k - 1] = block[:80].astype(jnp.bfloat16)
            c = remote(x_out.at[k - 1], x_in.at[k - 1], x_sems.at[0, k - 1], x_sems.at[1, k - 1], {"x": q})
            c.start()
            x_copies.append(c)
        else:
            total = block[:80]
    for c in x_copies:
        c.wait_recv()
    for k in range(3):
        total = total + x_in[k].astype(jnp.float32)
    out[...] = total * (-1.0 / math.sqrt(3072))

    for _, _, c in swaps:
        c.wait_send()
    for c in z_copies + zh_copies + x_copies:
        c.wait_send()
    for t in range(3):
        for hop in (1, 2, 3, 4):
            ring(t, 1, hop).wait_send()
            ring(t, -1, hop).wait_send()

    def rows_left(i):
        for t in range(3):
            for step in range(8):
                n = t * 8 + step
                s = slot(t, step)
                remote(rows.at[s], rows.at[s], row_out_sems.at[n, i], row_sems.at[n], other).wait_send()

    @pl.when(on_chain)
    def _():
        rows_left(0)

    @pl.when(on_chain & (zl >= home) & (zl < 3))
    def _():
        rows_left(1)

    @pl.when(on_chain & (zl <= home) & (zl > 0))
    def _():
        rows_left(2)


def exchange_scratch():
    dma = pltpu.SemaphoreType.DMA
    return [
        pltpu.VMEM((4, 32, WIDE), jnp.bfloat16),
        pltpu.VMEM((3, 32, WIDE), jnp.bfloat16),
        pltpu.VMEM((3, 32, WIDE), jnp.bfloat16),
        pltpu.VMEM((24, 32, WIDE), jnp.bfloat16),
        pltpu.VMEM((24, 32, 512), jnp.bfloat16),
        pltpu.VMEM((3, 80, WIDE), jnp.bfloat16),
        pltpu.VMEM((3, 80, WIDE), jnp.bfloat16),
        dma((2, 4)), dma((2, 3)), dma((2, 2)), dma((2, 24)), dma((24,)), dma((24, 3)), dma((2, 3)),
    ]


def exchange(parts, val_energy, cond_energy, occupation):
    return pl.pallas_call(
        exchange_body,
        out_shape=jax.ShapeDtypeStruct((80, WIDE), jnp.float32),
        in_specs=[pl.BlockSpec(memory_space=pltpu.VMEM)] * 4,
        out_specs=pl.BlockSpec(memory_space=pltpu.VMEM),
        scratch_shapes=exchange_scratch(),
        compiler_params=pltpu.CompilerParams(collective_id=0, has_side_effects=True, vmem_limit_bytes=32 * 2**20),
        name="exchange",
    )(parts, val_energy, cond_energy, occupation)


def body(valence, conduction, val_energy, cond_energy, val_occupation, gvectors):
    parts = partial_sums(valence, conduction, gvectors)
    chi = exchange(parts, val_energy.reshape(1, 16), cond_energy.reshape(1, 192), val_occupation.reshape(1, 16))
    return jnp.concatenate([chi[:, SUB * q : SUB * q + 240] for q in range(4)], axis=1)


def solution(mesh):
    finer = Mesh(mesh.devices.reshape(8, 4, 4, 2, 3), MESH_AXES)
    grow = ("zl", "core")
    bands = ("y", "x", "zh")
    placed = (P(None, grow, None), P(bands, grow, None), P(), P(), P(), P())
    return jax.shard_map(body, mesh=finer, in_specs=placed, out_specs=P(bands, grow), check_vma=False)
```

time: 158 us -> 117 us (0.74)
  the two profiles are of different devices: /device:TPU:4 before, /device:TPU:57 now
where the time goes in v2:
time: 117 us
  Pallas kernels  109 us (93%)
  local copies, waits for them, and re-layouts  6.56 us (6%)
    pallas_call x1, Pallas kernels, exchange(): pl.pallas_call(exchange_body, out_shape=jax.ShapeDtypeStruct((80, WIDE),...  95.8 us
    pallas_call x1, Pallas kernels, partial_sums(): pl.pallas_call(transform_body, out_shape=jax.ShapeDtypeStruct((4, 2, 32,...  13.7 us
    unnamed x18, local copies, waits for them, and re-layouts  6.54 us

profile of v2, /device:TPU:57, one launch (start us, length us, event | category | flops | bytes accessed | tf_op | source)
XLA Modules:
  0.0 116.9 jit_solution(15735274192043031483)
XLA Ops:
  0.0 0.0 copy-start.8
  0.0 0.0 copy-start.6
  0.0 0.0 copy-start.7
  0.0 0.0 copy-start
  0.0 2.0 %copy-done = bf16[16,12,9216]{2,0,1:T(8,128)(2,1)S(1)} copy-done((bf16[16,12,9216]{2,0,1:T(8,128)(2,1)S(1)}, bf16[16,12,9216]{2,0,1:T(8,128)(2,1)}, u32[]{:S(2)}) %copy-start) | copy-done | bytes 3538968
  2.0 0.0 copy-start.1
  2.1 1.0 copy-done.1
  3.1 0.0 copy-start.2
  3.1 0.9 copy-done.2
  4.0 0.0 copy-start.3
  4.0 0.9 copy-done.3
  4.9 0.0 copy-start.4
  4.9 0.8 copy-done.4
  5.7 0.0 copy-start.5
  5.7 0.8 copy-done.5
  6.5 13.7 %transform.1.parts = bf16[4,2,32,1024]{3,2,1,0:T(8,128)(2,1)S(1)} custom-call(bf16[12,16,9216]{2,1,0:T(8,128)(2,1)S(1)} %bitcast.5, bf16[12,2,9216]{2,1,0:T(2,128)(2,1)S(1)} %bitcast.6, s32[3,3840]{1,0:T(4,128)S(1)} %copy-done.5, f32[2,2,96,128]{3,2,1,0:T(8,128)S(1)} %copy-done.2, f32[5,2,12,128]{3,2,1,0:T(8,128)S(1)} %copy-done.3, ...), custom_call_target="tpu_custom_call" | custom-call | tf_op jit(solution)/shard_map/transform/pallas_call | solution.py:146
  20.2 0.0 copy-done.8
  20.2 0.0 copy-done.6
  20.3 0.0 copy-done.7
  20.3 95.8 %exchange.1 = f32[80,1024]{1,0:T(8,128)S(1)} custom-call(bf16[4,2,32,1024]{3,2,1,0:T(8,128)(2,1)S(1)} %transform.1.parts, f32[1,16]{1,0:T(1,128)S(1)} %bitcast.8, f32[1,192]{1,0:T(1,128)S(1)} %bitcast.7, s32[1,16]{1,0:T(1,128)S(1)} %bitcast.9), custom_call_target="tpu_custom_call" | custom-call | tf_op jit(solution)/shard_map/exchange/pallas_call | solution.py:384
  116.1 0.9 pad_maximum_fusion
  (1 shorter events, 0.0 us)
Async XLA Ops:
  0.0 20.2 %copy-start.8 = (s32[16]{0:T(128)S(1)}, s32[16]{0:T(128)}, u32[]{:S(2)}) copy-start(s32[16]{0:T(128)} %param.13) | copy-start | bytes 196
  0.0 20.2 %copy-start.6 = (f32[192]{0:T(256)S(1)}, f32[192]{0:T(256)}, u32[]{:S(2)}) copy-start(f32[192]{0:T(256)} %param.12) | copy-start | bytes 2308
  0.0 20.2 %copy-start.7 = (f32[16]{0:T(128)S(1)}, f32[16]{0:T(128)}, u32[]{:S(2)}) copy-start(f32[16]{0:T(128)} %param.11) | copy-start | bytes 196
  0.0 2.0 %copy-start = (bf16[16,12,9216]{2,0,1:T(8,128)(2,1)S(1)}, bf16[16,12,9216]{2,0,1:T(8,128)(2,1)}, u32[]{:S(2)}) copy-start(bf16[16,12,9216]{2,0,1:T(8,128)(2,1)} %param.9) | copy-start | bytes 10616836
  2.0 1.0 copy-start.1
  3.1 0.9 copy-start.2
  4.0 0.9 copy-start.3
  4.9 0.8 copy-start.4
  5.7 0.8 copy-start.5

commit v3 on v2

--- a/solution.py
+++ b/solution.py
@@ -149,7 +149,7 @@
         in_specs=[pl.BlockSpec(memory_space=pl.ANY)] * 6,
         out_specs=pl.BlockSpec(memory_space=pltpu.VMEM),
         scratch_shapes=transform_scratch(),
-        compiler_params=pltpu.CompilerParams(vmem_limit_bytes=48 * 2**20),
+        compiler_params=pltpu.CompilerParams(vmem_limit_bytes=60 * 2**20),
         name="transform",
     )(valence.transpose(1, 0, 2), conduction.transpose(1, 0, 2), gvectors,
       jnp.asarray(z_tab), jnp.asarray(y_tab), jnp.asarray(x_tab, jnp.bfloat16))
@@ -183,7 +183,7 @@
 
 
 def exchange_body(parts, val_energy, cond_energy, occupation, out,
-                  core_in, z_out, z_in, cols, rows, x_out, x_in,
+                  core_in, z_out, z_in, cols, rows, blocks, x_out, x_in,
                   core_sems, z_sems, zh_sems, y_sems, row_sems, row_out_sems, x_sems):
     y, x, zl, core, zh = (lax.axis_index(a) for a in MESH_AXES)
     barrier = pltpu.get_barrier_semaphore()
@@ -234,40 +234,39 @@
     def slot(t, step):
         return turned("zh", -t) * 8 + turned("y", step)
 
-    def pick_rows(s):
-        here = lax.broadcasted_iota(jnp.int32, (SUB, 128), 0)
-        there = lax.broadcasted_iota(jnp.int32, (SUB, 128), 1)
-        pick = ((here == there + 80 * zh) & (there < 80)).astype(jnp.float32).astype(jnp.bfloat16)
-        for q in range(4):
-            cut = jnp.dot(cols[s, :, SUB * q : SUB * (q + 1)], pick, preferred_element_type=jnp.float32)
-            rows[s, :, 128 * q : 128 * (q + 1)] = cut.astype(jnp.bfloat16)
-
-    def pass_rows(t, step):
+    def row_copy(n, s, i, target):
+        return remote(rows.at[s], rows.at[s], row_out_sems.at[n, i], row_sems.at[n], target)
+
+    def give_rows(t, step):
         n = t * 8 + step % 8
         s = slot(t, step)
 
-        def send(i, target):
-            remote(rows.at[s], rows.at[s], row_out_sems.at[n, i], row_sems.at[n], target).start()
-
         @pl.when(source)
         def _():
-            pick_rows(s)
-
-        @pl.when(jnp.logical_not(source))
+            for third in range(3):
+
+                @pl.when(zh == third)
+                def _():
+                    for q in range(4):
+                        rows[s, :, 80 * q : 80 * q + 80] = cols[s, :, SUB * q + 80 * third : SUB * q + 80 * third + 80]
+
+            for k in (3, 2, 1):
+                row_copy(n, s, k - 1, {"zl": turned("zl", k)}).start()
+            row_copy(n, s, 3, other).start()
+
+    def relay_rows(t, step):
+        n = t * 8 + step % 8
+        s = slot(t, step)
+
+        @pl.when(on_chain & (zl != home))
         def _():
-            remote(rows.at[s], rows.at[s], row_out_sems.at[n, 0], row_sems.at[n], other).wait_recv()
-
-        @pl.when(on_chain)
-        def _():
-            send(0, other)
-
-        @pl.when(on_chain & (zl >= home) & (zl < 3))
-        def _():
-            send(1, {"zl": lax.rem(zl + 1, 4)})
-
-        @pl.when(on_chain & (zl <= home) & (zl > 0))
-        def _():
-            send(2, {"zl": lax.rem(zl + 3, 4)})
+            row_copy(n, s, 3, other).wait_recv()
+            row_copy(n, s, 3, other).start()
+
+    def row_waits(act):
+        for t in range(3):
+            for step in range(8):
+                act(t * 8 + step, slot(t, step))
 
     def ring(t, way, hop):
         s = slot(t, -way * (hop - 1))
@@ -288,22 +287,27 @@
         ring(t, -1, hop).start()
 
     start(0, 1)
-    pass_rows(0, 0)
+    give_rows(0, 0)
     for hop in (1, 2, 3):
         landed(0, 1, hop)
         ring(0, 1, hop + 1).start()
         landed(0, -1, hop)
         ring(0, -1, hop + 1).start()
-        pass_rows(0, -hop)
-        pass_rows(0, hop)
-    for t in (1, 2):
-        zh_copies[t - 1].wait_recv()
-        start(t, 1)
-    for t in (1, 2):
-        pass_rows(t, 0)
+        give_rows(0, -hop)
+        give_rows(0, hop)
+        if hop == 2:
+            for t in (1, 2):
+                zh_copies[t - 1].wait_recv()
+                start(t, 1)
+            for t in (1, 2):
+                give_rows(t, 0)
+    for step in (0, 1, -1, 2, -2):
+        relay_rows(0, step)
     landed(0, 1, 4)
     landed(0, -1, 4)
-    pass_rows(0, 4)
+    give_rows(0, 4)
+    for t in (1, 2):
+        relay_rows(t, 0)
     for hop in (1, 2, 3):
         for t in (1, 2):
             landed(t, 1, hop)
@@ -311,26 +315,38 @@
             landed(t, -1, hop)
             ring(t, -1, hop + 1).start()
         for t in (1, 2):
-            pass_rows(t, -hop)
-            pass_rows(t, hop)
+            give_rows(t, -hop)
+            give_rows(t, hop)
+        if hop == 1:
+            for step in (3, -3, 4):
+                relay_rows(0, step)
+        else:
+            for t in (1, 2):
+                relay_rows(t, hop - 1)
+                relay_rows(t, 1 - hop)
     for t in (1, 2):
         landed(t, 1, 4)
         landed(t, -1, 4)
-        pass_rows(t, 4)
-
+        give_rows(t, 4)
+    for t in (1, 2):
+        for step in (3, -3, 4):
+            relay_rows(t, step)
+
+    @pl.when(jnp.logical_not(on_chain))
+    def _():
+        row_waits(lambda n, s: row_copy(n, s, 3, other).wait_recv())
+
+    left = rows[:, :, 0:320].reshape(768, 320)
     right = cols[...].reshape(768, WIDE)
+    blocks[...] = lax.dot_general(left, right, (((0,), (0,)), ((), ())), preferred_element_type=jnp.float32)
     x_copies = []
-    for k in (2, 1, 3, 0):
+    for k in (2, 1, 3):
         q = turned("x", k)
-        left = rows[:, :, pl.ds(pl.multiple_of(128 * q, 128), 128)].reshape(768, 128)
-        block = lax.dot_general(left, right, (((0,), (0,)), ((), ())), preferred_element_type=jnp.float32)
-        if k:
-            x_out[k - 1] = block[:80].astype(jnp.bfloat16)
-            c = remote(x_out.at[k - 1], x_in.at[k - 1], x_sems.at[0, k - 1], x_sems.at[1, k - 1], {"x": q})
-            c.start()
-            x_copies.append(c)
-        else:
-            total = block[:80]
+        x_out[k - 1] = blocks[pl.ds(pl.multiple_of(80 * q, 80), 80)].astype(jnp.bfloat16)
+        c = remote(x_out.at[k - 1], x_in.at[k - 1], x_sems.at[0, k - 1], x_sems.at[1, k - 1], {"x": q})
+        c.start()
+        x_copies.append(c)
+    total = blocks[pl.ds(pl.multiple_of(80 * x, 80), 80)]
     for c in x_copies:
         c.wait_recv()
     for k in range(3):
@@ -346,24 +362,14 @@
             ring(t, 1, hop).wait_send()
             ring(t, -1, hop).wait_send()
 
-    def rows_left(i):
-        for t in range(3):
-            for step in range(8):
-                n = t * 8 + step
-                s = slot(t, step)
-                remote(rows.at[s], rows.at[s], row_out_sems.at[n, i], row_sems.at[n], other).wait_send()
-
-    @pl.when(on_chain)
+    @pl.when(source)
     def _():
-        rows_left(0)
-
-    @pl.when(on_chain & (zl >= home) & (zl < 3))
+        for i in range(4):
+            row_waits(lambda n, s: row_copy(n, s, i, other).wait_send())
+
+    @pl.when(on_chain & (zl != home))
     def _():
-        rows_left(1)
-
-    @pl.when(on_chain & (zl <= home) & (zl > 0))
-    def _():
-        rows_left(2)
+        row_waits(lambda n, s: row_copy(n, s, 3, other).wait_send())
 
 
 def exchange_scratch():
@@ -373,10 +379,11 @@
         pltpu.VMEM((3, 32, WIDE), jnp.bfloat16),
         pltpu.VMEM((3, 32, WIDE), jnp.bfloat16),
         pltpu.VMEM((24, 32, WIDE), jnp.bfloat16),
-        pltpu.VMEM((24, 32, 512), jnp.bfloat16),
+        pltpu.VMEM((24, 32, 384), jnp.bfloat16),
+        pltpu.VMEM((320, WIDE), jnp.float32),
         pltpu.VMEM((3, 80, WIDE), jnp.bfloat16),
         pltpu.VMEM((3, 80, WIDE), jnp.bfloat16),
-        dma((2, 4)), dma((2, 3)), dma((2, 2)), dma((2, 24)), dma((24,)), dma((24, 3)), dma((2, 3)),
+        dma((2, 4)), dma((2, 3)), dma((2, 2)), dma((2, 24)), dma((24,)), dma((24, 4)), dma((2, 3)),
     ]
 
 
@@ -387,7 +394,7 @@
         in_specs=[pl.BlockSpec(memory_space=pltpu.VMEM)] * 4,
         out_specs=pl.BlockSpec(memory_space=pltpu.VMEM),
         scratch_shapes=exchange_scratch(),
-        compiler_params=pltpu.CompilerParams(collective_id=0, has_side_effects=True, vmem_limit_bytes=32 * 2**20),
+        compiler_params=pltpu.CompilerParams(collective_id=0, has_side_effects=True, vmem_limit_bytes=60 * 2**20),
         name="exchange",
     )(parts, val_energy, cond_energy, occupation)
 

time: 117 us -> 85.7 us (0.73)
  the two profiles are of different devices: /device:TPU:57 before, /device:TPU:65 now
where the time goes in v3:
time: 85.7 us; the launch traced here: 85.5 us
  Pallas kernels  83.6 us (98%)
  local copies, waits for them, and re-layouts  1.03 us (1%)
  other arithmetic  0.89 us (1%)
    pallas_call x1, Pallas kernels, exchange(): pl.pallas_call(exchange_body, out_shape=jax.ShapeDtypeStruct((80, WIDE),...  69.8 us
    pallas_call x1, Pallas kernels, partial_sums(): pl.pallas_call(transform_body, out_shape=jax.ShapeDtypeStruct((4, 2, 32,...  13.8 us

profile of v3, /device:TPU:65, one launch (start us, length us, event | category | flops | bytes accessed | tf_op | source)
XLA Modules:
  0.0 85.5 jit_solution(8328822049358825931)
XLA Ops:
  0.0 13.8 %transform.1.parts = bf16[4,2,32,1024]{3,2,1,0:T(8,128)(2,1)} custom-call(bf16[12,16,9216]{2,1,0:T(8,128)(2,1)} %bitcast.5, bf16[12,2,9216]{2,1,0:T(2,128)(2,1)} %bitcast.6, s32[3,3840]{1,0:T(4,128)} %gvec_in.1, f32[2,2,96,128]{3,2,1,0:T(8,128)} %constant.6.clone.z_in, f32[5,2,12,128]{3,2,1,0:T(8,128)} %constant.7.clone.y_in, ...), custom_call_target="tpu_custom_call" | custom-call | tf_op jit(solution)/shard_map/transform/pallas_call | solution.py:146
  13.8 69.8 %exchange.1 = f32[80,1024]{1,0:T(8,128)} custom-call(bf16[4,2,32,1024]{3,2,1,0:T(8,128)(2,1)} %transform.1.parts, f32[1,16]{1,0:T(1,128)} %bitcast.8, f32[1,192]{1,0:T(1,128)} %bitcast.7, s32[1,16]{1,0:T(1,128)} %bitcast.9), custom_call_target="tpu_custom_call" | custom-call | tf_op jit(solution)/shard_map/exchange/pallas_call | solution.py:391
  83.6 1.0 %fusion = (f32[80,240]{1,0:T(8,128)S(1)}, f32[80,240]{1,0:T(8,128)S(1)}, f32[80,240]{1,0:T(8,128)S(1)}, f32[80,240]{1,0:T(8,128)S(1)}) fusion(f32[80,1024]{1,0:T(8,128)} %exchange.1), kind=kLoop, calls=%fused_computation.1 | loop fusion | bytes 614400 | tf_op jit(solution)/shard_map/slice | solution.py:405
  84.6 0.9 %pad_maximum_fusion = f32[80,960]{1,0:T(8,128)} fusion(f32[80,240]{1,0:T(8,128)S(1)} %get-tuple-element.6, f32[80,240]{1,0:T(8,128)S(1)} %get-tuple-element.7, f32[80,240]{1,0:T(8,128)S(1)} %get-tuple-element.8, f32[80,240]{1,0:T(8,128)S(1)} %get-tuple-element.5), kind=kLoop, calls=%fused_computation | loop fusion | flops 230400 | bytes 614400 | tf_op jit(solution)/shard_map/concatenate | solution.py:405

commit v4 on v3

v4 whole, which is shorter than its diff:
```python
import functools
import math

import jax
import jax.numpy as jnp
import numpy as np
from jax import lax
from jax.experimental import pallas as pl
from jax.experimental.pallas import tpu as pltpu
from jax.sharding import Mesh
from jax.sharding import PartitionSpec as P

N=96; RAD=12; KG=3840; NV=16
PL=12
PART=1152
HALF=math.sqrt(0.5)

def lane_waves():
    j=np.zeros((4,128),np.int64); k=np.zeros((4,128),np.int64); used=np.zeros((4,2,128))
    for l in range(91):
        j[0,l],k[0,l]=(-8+8*(l//13),l%13) if l<39 else (-12+8*((l-39)//13),(l-39)%13)
        used[0,0 if l<39 else 1,l]=1
    for c in (1,2,3):
        for l in range(75):
            j[c,l],k[c,l]=c-8+8*(l//25),l%25-12
            used[c,:,l]=1
    return j,k,used

def phase_of(n): return 2*np.pi*np.mod(n,N)/N

def tables():
    j,k,used=lane_waves()
    z=np.arange(N); y=np.arange(12)
    kz=phase_of(z[None,:,None]*k[:2,None,:])
    z_tab=np.stack([np.cos(kz),np.sin(kz)],1).astype(np.float32)
    jy=phase_of(y[None,:,None]*j[:,None,:])
    y_tab=np.stack([np.cos(jy),np.sin(jy)],1)
    first=np.where(used[:,0,None,None,:]>0,y_tab,0.0)
    y_tab0=np.where(used[0,1,None,None,:]>0,y_tab[0],0.0)
    y_all=np.concatenate([first,y_tab0[None]],0).astype(np.float32)
    a=np.arange(16)
    X=np.arange(N).reshape(8,12)
    ax=phase_of(X[:,:,None]*a[None,None,:])
    x_tab=np.zeros((8,32,16),np.float32)
    x_tab[:,:12]=np.cos(ax); x_tab[:,16:28]=np.sin(ax)
    return z_tab,y_all,x_tab

def sections(val, con, gvec_in, z_in, y_in, x_in, vbuf, cbuf, gvec, z_tab, y_tab, x_tab, tab, mixed, sec_re, sec_im, keys, sems):
    grow=2*lax.axis_index("zl")+lax.axis_index("core")
    small=[pltpu.make_async_copy(a,b,sems.at[8+i]) for i,(a,b) in enumerate([(z_in,z_tab),(y_in,y_tab),(gvec_in,gvec),(x_in.at[grow],x_tab)])]
    for c in small: c.start()
    copies=[]
    for s in range(4):
        copies.append((pltpu.make_async_copy(val.at[pl.ds(3*s,3)],vbuf.at[pl.ds(3*s,3)],sems.at[s]),
                       pltpu.make_async_copy(con.at[pl.ds(3*s,3)],cbuf.at[pl.ds(3*s,3)],sems.at[4+s])))
    for pair in copies:
        for c in pair: c.start()
    for c in small: c.wait()
    with jax.named_scope("tables"):
        def build(yp,_):
            row=pl.ds(pl.multiple_of(yp*N,32),N)
            for t in range(4):
                cz=z_tab[min(t,1),0]; sz=z_tab[min(t,1),1]
                cy=y_tab[t,0,pl.ds(yp,1)]; sy=y_tab[t,1,pl.ds(yp,1)]
                co=(cy*cz-sy*sz); si=(sy*cz+cy*sz)
                tab[t,row,0:128]=co.astype(jnp.bfloat16)
                tab[t,row,128:256]=si.astype(jnp.bfloat16)
                row2=pl.ds(pl.multiple_of(PART+yp*N,32),N)
                if t==0:
                    cy=y_tab[4,0,pl.ds(yp,1)]; sy=y_tab[4,1,pl.ds(yp,1)]
                    tab[t,row2,0:128]=(cy*cz-sy*sz).astype(jnp.bfloat16)
                    tab[t,row2,128:256]=(sy*cz+cy*sz).astype(jnp.bfloat16)
                else:
                    tab[t,row2,0:128]=(-si).astype(jnp.bfloat16)
                    tab[t,row2,128:256]=co.astype(jnp.bfloat16)
            return 0
        lax.fori_loop(0,12,build,0)
    keys[...] = jnp.zeros_like(keys)
    for b in range(16):
        lanes=pl.ds(240*b,240)
        a=gvec[0:1,lanes]; j=gvec[1:2,lanes]; k=gvec[2:3,lanes]
        j8=j&7
        flip=(j8>=5)|(((j8&3)==0)&((k<0)|((k==0)&(j<0))))
        j=jnp.where(flip,-j,j); k=jnp.where(flip,-k,k)
        c=j&7
        odd=128*c+25*((j+8-c)>>3)+k+12
        even=jnp.where(c==0,13*((j+8)>>3)+k,39+13*((j+12)>>3)+k)
        lanes=pl.ds(256*(b%4),240)
        keys[b//4,0:1,lanes]=jnp.where((c&3)==0,even,odd)
        keys[b//4,1:2,lanes]=a
        keys[b//4,2:3,lanes]=flip.astype(jnp.int32)
    with jax.named_scope("mix"):
        def mix(x,_):
            for c in range(2):
                row=pl.ds(pl.multiple_of(x*32+16*c,16),16)
                for w in range(0,PART,384):
                    d=[]
                    for q in range(8):
                        lanes=pl.ds(q*PART+w,384)
                        d.append((vbuf[x,:,lanes]*cbuf[x,c:c+1,lanes]).astype(jnp.float32))
                    a=[d[q]+d[q+4] for q in range(4)]
                    m=[d[q]-d[q+4] for q in range(4)]
                    p=(m[1]-m[3])*HALF; r=(m[1]+m[3])*HALF
                    even=a[0]+a[2]; odd=a[1]+a[3]
                    for t,(u,v) in enumerate([(even+odd,even-odd),(m[0]+p,m[2]+r),(a[0]-a[2],a[1]-a[3]),(m[0]-p,r-m[2])]):
                        mixed[t,row,w:w+384]=u.astype(jnp.bfloat16)
                        mixed[t,row,PART+w:PART+w+384]=v.astype(jnp.bfloat16)
            return 0
        for s in range(4):
            for c in copies[s]: c.wait()
            lax.fori_loop(3*s,3*s+3,mix,0)
    with jax.named_scope("planes"):
        for t in range(4):
            both=jnp.dot(mixed[t],tab[t],preferred_element_type=jnp.float32)
            sec_re[:,128*t:128*(t+1)]=both[:,:128].astype(jnp.bfloat16)
            sec_im[:,128*t:128*(t+1)]=both[:,128:].astype(jnp.bfloat16)

def pick(b, out, x_tab, sec_re, sec_im, keys):
    waves=x_tab[...]
    for n0 in range(0,1024,256):
        w=256
        lanes=pl.ds(n0,w)
        rho=keys[b,0:1,lanes]; a=keys[b,1:2,lanes]; sign=1.0-2.0*keys[b,2:3,lanes].astype(jnp.float32)
        hot=(lax.broadcasted_iota(jnp.int32,(512,w),0)==rho).astype(jnp.float32).astype(jnp.bfloat16)
        hot_a=(lax.broadcasted_iota(jnp.int32,(16,w),0)==a).astype(jnp.float32).astype(jnp.bfloat16)
        wave=jnp.dot(waves,hot_a,preferred_element_type=jnp.float32)
        re=jnp.dot(sec_re[...],hot,preferred_element_type=jnp.float32)
        im=jnp.dot(sec_im[...],hot,preferred_element_type=jnp.float32)
        tot_re=jnp.zeros((32,w),jnp.float32); tot_im=jnp.zeros((32,w),jnp.float32)
        for x in range(PL):
            co=wave[x:x+1]; si=wave[16+x:17+x]
            gr=re[32*x:32*x+32]; gi=im[32*x:32*x+32]
            tot_re+=co*gr-(si*sign)*gi
            tot_im+=si*gr+(co*sign)*gi
        out[b//2,lax.rem(b,2),:,lanes]=tot_re.astype(out.dtype)
        out[2+b//2,lax.rem(b,2),:,lanes]=(-tot_im).astype(out.dtype)


MESH_AXES = ("y", "x", "zl", "core", "zh")
SIDE = pl.DeviceIdType.MESH
SUB = 256
WIDE = 4 * SUB


def turned(axis, step):
    size = lax.axis_size(axis)
    return lax.rem(lax.axis_index(axis) + step % size, size)


def remote(src, dst, send_sem, recv_sem, target):
    return pltpu.make_async_remote_copy(src_ref=src, dst_ref=dst, send_sem=send_sem, recv_sem=recv_sem,
                                        device_id=target, device_id_type=SIDE)


def pair_factor(val_energy, cond_energy, occupation):
    first = ((lax.axis_index("y") * 4 + lax.axis_index("x")) * 3 + lax.axis_index("zh")) * 2
    row = lax.broadcasted_iota(jnp.int32, (32, 16), 0)
    at_v = lax.broadcasted_iota(jnp.int32, (32, 16), 1) == (row & 15)
    ev = jnp.sum(jnp.where(at_v, val_energy, 0.0), axis=1, keepdims=True)
    occ = jnp.sum(jnp.where(at_v, occupation.astype(jnp.float32), 0.0), axis=1, keepdims=True)
    row = lax.broadcasted_iota(jnp.int32, (32, 192), 0)
    at_c = lax.broadcasted_iota(jnp.int32, (32, 192), 1) == first + (row >> 4)
    ec = jnp.sum(jnp.where(at_c, cond_energy, 0.0), axis=1, keepdims=True)
    return jnp.sqrt(occ / (4.0 * (ec - ev))) * (1.0 / N**1.5)


def fused_body(val, con, gvec_in, z_tab_in, y_tab_in, x_tab_in, val_energy, cond_energy, occupation, out,
                  vbuf, cbuf, gvec, z_tab, y_tab, x_tab, tab, mixed, sec_re, sec_im, keys, load_sems, parts,
                  core_in, z_out, z_in, cols, rows, blocks, x_out, x_in,
                  core_sems, z_sems, zh_sems, y_sems, row_sems, row_out_sems, x_sems):
    y, x, zl, core, zh = (lax.axis_index(a) for a in MESH_AXES)
    barrier = pltpu.get_barrier_semaphore()
    partners = ([{"core": 1 - core}] + [{"zl": turned("zl", k)} for k in (1, 2, 3)]
                + [{"zh": turned("zh", k)} for k in (1, 2)] + [{"y": turned("y", k)} for k in (1, 7)]
                + [{"x": turned("x", k)} for k in (1, 2, 3)])
    for target in partners:
        pl.semaphore_signal(barrier, inc=1, device_id=target, device_id_type=SIDE)

    sections(val, con, gvec_in, z_tab_in, y_tab_in, x_tab_in, vbuf, cbuf, gvec, z_tab, y_tab, x_tab, tab, mixed,
             sec_re, sec_im, keys, load_sems)
    with jax.named_scope("barrier"):
        pl.semaphore_wait(barrier, len(partners))

    other = {"core": 1 - core}
    odd = 1 - lax.rem(zl, 2)

    def swap(k):
        return remote(parts.at[turned("zl", k), 1 - core], core_in.at[k], core_sems.at[0, k], core_sems.at[1, k], other)

    def pass_on(k):
        return remote(z_out.at[k - 1], z_in.at[k - 1], z_sems.at[0, k - 1], z_sems.at[1, k - 1], {"zl": turned("zl", k)})

    def both_cores(k):
        swap(k).wait_recv()
        return parts[turned("zl", k), core].astype(jnp.float32) + core_in[k].astype(jnp.float32)

    with jax.named_scope("picks"):
        pick(2 * odd + 1 - core, parts, x_tab, sec_re, sec_im, keys)
        for k in (1, 3):
            swap(k).start()
        pick(2 * (1 - odd) + 1 - core, parts, x_tab, sec_re, sec_im, keys)
        for k in (2, 0):
            swap(k).start()
        pick(2 * odd + core, parts, x_tab, sec_re, sec_im, keys)
        for k in (1, 3):
            z_out[k - 1] = both_cores(k).astype(jnp.bfloat16)
            pass_on(k).start()
        pick(2 * (1 - odd) + core, parts, x_tab, sec_re, sec_im, keys)
        z_out[1] = both_cores(2).astype(jnp.bfloat16)
        pass_on(2).start()
        total = both_cores(0)
    factor = pair_factor(val_energy[...], cond_energy[...], occupation[...])
    with jax.named_scope("zsum"):
        for k in (1, 3, 2):
            pass_on(k).wait_recv()
            total = total + z_in[k - 1].astype(jnp.float32)
    mine = zh * 8 + y
    cols[mine] = (total * factor).astype(jnp.bfloat16)

    zh_copies = []
    for k in (1, 2):
        c = remote(cols.at[mine], cols.at[mine], zh_sems.at[0, k - 1], zh_sems.at[1, k - 1], {"zh": turned("zh", k)})
        c.start()
        zh_copies.append(c)

    plane = 2 * zl + core
    home = y // 2
    on_chain = core == lax.rem(y, 2)
    source = plane == y

    def slot(t, step):
        return turned("zh", -t) * 8 + turned("y", step)

    def row_copy(n, s, i, target):
        return remote(rows.at[s], rows.at[s], row_out_sems.at[n, i], row_sems.at[n], target)

    def give_rows(t, step):
        n = t * 8 + step % 8
        s = slot(t, step)

        @pl.when(source)
        def _():
            for third in range(3):

                @pl.when(zh == third)
                def _():
                    for q in range(4):
                        rows[s, :, 80 * q : 80 * q + 80] = cols[s, :, SUB * q + 80 * third : SUB * q + 80 * third + 80]

            for k in (3, 2, 1):
                row_copy(n, s, k - 1, {"zl": turned("zl", k)}).start()
            row_copy(n, s, 3, other).start()

    def relay_rows(t, step):
        n = t * 8 + step % 8
        s = slot(t, step)

        @pl.when(on_chain & (zl != home))
        def _():
            row_copy(n, s, 3, other).wait_recv()
            row_copy(n, s, 3, other).start()

    def row_waits(act):
        for t in range(3):
            for step in range(8):
                act(t * 8 + step, slot(t, step))

    def ring(t, way, hop):
        s = slot(t, -way * (hop - 1))
        d = 0 if way == 1 else 1
        n = (t * 4 + hop - 1) * 2 + d
        half = pl.ds(0, 32) if hop < 4 else pl.ds(16 * d, 16)
        return remote(cols.at[s, half], cols.at[s, half], y_sems.at[0, n], y_sems.at[1, n], {"y": turned("y", way)})

    def landed(t, way, hop):
        s = slot(t, -way * hop)
        d = 0 if way == 1 else 1
        n = (t * 4 + hop - 1) * 2 + d
        half = pl.ds(0, 32) if hop < 4 else pl.ds(16 * d, 16)
        remote(cols.at[s, half], cols.at[s, half], y_sems.at[0, n], y_sems.at[1, n], {"y": turned("y", way)}).wait_recv()

    def start(t, hop):
        ring(t, 1, hop).start()
        ring(t, -1, hop).start()

    with jax.named_scope("ring0"):
        start(0, 1)
        give_rows(0, 0)
        for hop in (1, 2, 3):
            landed(0, 1, hop)
            ring(0, 1, hop + 1).start()
            landed(0, -1, hop)
            ring(0, -1, hop + 1).start()
            give_rows(0, -hop)
            give_rows(0, hop)
            if hop == 2:
                for t in (1, 2):
                    with jax.named_scope("zh"):
                        zh_copies[t - 1].wait_recv()
                    start(t, 1)
                for t in (1, 2):
                    give_rows(t, 0)
    with jax.named_scope("relay0"):
        for step in (0, 1, -1, 2, -2):
            relay_rows(0, step)
    with jax.named_scope("ring04"):
        landed(0, 1, 4)
        landed(0, -1, 4)
        give_rows(0, 4)
        for t in (1, 2):
            relay_rows(t, 0)
    for hop in (1, 2, 3):
        for t in (1, 2):
            with jax.named_scope("ring%d%d" % (t, hop)):
                landed(t, 1, hop)
                ring(t, 1, hop + 1).start()
                landed(t, -1, hop)
                ring(t, -1, hop + 1).start()
        for t in (1, 2):
            give_rows(t, -hop)
            give_rows(t, hop)
        if hop == 1:
            for step in (3, -3, 4):
                relay_rows(0, step)
        else:
            for t in (1, 2):
                relay_rows(t, hop - 1)
                relay_rows(t, 1 - hop)
    with jax.named_scope("ring124"):
        for t in (1, 2):
            landed(t, 1, 4)
            landed(t, -1, 4)
            give_rows(t, 4)
    with jax.named_scope("rowwait"):
        for t in (1, 2):
            for step in (3, -3, 4):
                relay_rows(t, step)

        @pl.when(jnp.logical_not(on_chain))
        def _():
            row_waits(lambda n, s: row_copy(n, s, 3, other).wait_recv())

    with jax.named_scope("matmul"):
        left = rows[:, :, 0:320].reshape(768, 320)
        right = cols[...].reshape(768, WIDE)
        blocks[...] = lax.dot_general(left, right, (((0,), (0,)), ((), ())), preferred_element_type=jnp.float32)
        x_copies = []
        for k in (2, 1, 3):
            q = turned("x", k)
            x_out[k - 1] = blocks[pl.ds(pl.multiple_of(80 * q, 80), 80)].astype(jnp.bfloat16)
            c = remote(x_out.at[k - 1], x_in.at[k - 1], x_sems.at[0, k - 1], x_sems.at[1, k - 1], {"x": q})
            c.start()
            x_copies.append(c)
        total = blocks[pl.ds(pl.multiple_of(80 * x, 80), 80)]
    with jax.named_scope("xsum"):
        for c in x_copies:
            c.wait_recv()
        for k in range(3):
            total = total + x_in[k].astype(jnp.float32)
    total = total * (-1.0 / math.sqrt(3072))
    for q in range(4):
        out[:, 240 * q : 240 * q + 240] = total[:, SUB * q : SUB * q + 240]

    for k in range(4):
        swap(k).wait_send()
    for k in (1, 2, 3):
        pass_on(k).wait_send()
    for c in zh_copies + x_copies:
        c.wait_send()
    for t in range(3):
        for hop in (1, 2, 3, 4):
            ring(t, 1, hop).wait_send()
            ring(t, -1, hop).wait_send()

    @pl.when(source)
    def _():
        for i in range(4):
            row_waits(lambda n, s: row_copy(n, s, i, other).wait_send())

    @pl.when(on_chain & (zl != home))
    def _():
        row_waits(lambda n, s: row_copy(n, s, 3, other).wait_send())


def fused_scratch():
    dma = pltpu.SemaphoreType.DMA
    return [
        pltpu.VMEM((PL, NV, 9216), jnp.bfloat16),
        pltpu.VMEM((PL, 2, 9216), jnp.bfloat16),
        pltpu.VMEM((3, KG), jnp.int32),
        pltpu.VMEM((2, 2, 96, 128), jnp.float32),
        pltpu.VMEM((5, 2, 12, 128), jnp.float32),
        pltpu.VMEM((32, 16), jnp.bfloat16),
        pltpu.VMEM((4, 2 * PART, 256), jnp.bfloat16),
        pltpu.VMEM((4, 384, 2 * PART), jnp.bfloat16),
        pltpu.VMEM((384, 512), jnp.bfloat16),
        pltpu.VMEM((384, 512), jnp.bfloat16),
        pltpu.VMEM((4, 8, 1024), jnp.int32),
        dma((12,)),
        pltpu.VMEM((4, 2, 32, WIDE), jnp.bfloat16),
        pltpu.VMEM((4, 32, WIDE), jnp.bfloat16),
        pltpu.VMEM((3, 32, WIDE), jnp.bfloat16),
        pltpu.VMEM((3, 32, WIDE), jnp.bfloat16),
        pltpu.VMEM((24, 32, WIDE), jnp.bfloat16),
        pltpu.VMEM((24, 32, 384), jnp.bfloat16),
        pltpu.VMEM((320, WIDE), jnp.float32),
        pltpu.VMEM((3, 80, WIDE), jnp.bfloat16),
        pltpu.VMEM((3, 80, WIDE), jnp.bfloat16),
        dma((2, 4)), dma((2, 3)), dma((2, 2)), dma((2, 24)), dma((24,)), dma((24, 4)), dma((2, 3)),
    ]


def body(valence, conduction, val_energy, cond_energy, val_occupation, gvectors):
    z_tab, y_tab, x_tab = tables()
    return pl.pallas_call(
        fused_body,
        out_shape=jax.ShapeDtypeStruct((80, 960), jnp.float32),
        in_specs=[pl.BlockSpec(memory_space=pl.ANY)] * 6 + [pl.BlockSpec(memory_space=pltpu.VMEM)] * 3,
        out_specs=pl.BlockSpec(memory_space=pltpu.VMEM),
        scratch_shapes=fused_scratch(),
        compiler_params=pltpu.CompilerParams(collective_id=0, has_side_effects=True, vmem_limit_bytes=60 * 2**20),
        name="chi",
    )(valence.transpose(1, 0, 2), conduction.transpose(1, 0, 2), gvectors,
      jnp.asarray(z_tab), jnp.asarray(y_tab), jnp.asarray(x_tab, jnp.bfloat16),
      val_energy.reshape(1, 16), cond_energy.reshape(1, 192), val_occupation.reshape(1, 16))


def solution(mesh):
    finer = Mesh(mesh.devices.reshape(8, 4, 4, 2, 3), MESH_AXES)
    grow = ("zl", "core")
    bands = ("y", "x", "zh")
    placed = (P(None, grow, None), P(bands, grow, None), P(), P(), P(), P())
    return jax.shard_map(body, mesh=finer, in_specs=placed, out_specs=P(bands, grow), check_vma=False)
```

time: 85.7 us -> 80.1 us (0.935)
  the two profiles are of different devices: /device:TPU:65 before, /device:TPU:17 now
where the time goes in v4:
time: 80.1 us; the launch traced here: 79.9 us
  Pallas kernels  78.1 us (98%)
  local copies, waits for them, and re-layouts  1.72 us (2%)
    pallas_call x1, Pallas kernels, body(): pl.pallas_call(fused_body, out_shape=jax.ShapeDtypeStruct((80, 960), jnp....  78.1 us
    unnamed x1, local copies, waits for them, and re-layouts  1.72 us

profile of v4, /device:TPU:17, one launch (start us, length us, event | category | flops | bytes accessed | tf_op | source)
XLA Modules:
  0.0 79.9 jit_solution(2345266038428077098)
XLA Ops:
  0.0 78.1 %chi.1 = f32[80,960]{1,0:T(8,128)} custom-call(bf16[12,16,9216]{2,1,0:T(8,128)(2,1)} %bitcast.5, bf16[12,2,9216]{2,1,0:T(2,128)(2,1)} %bitcast.6, s32[3,3840]{1,0:T(4,128)} %gvec_in.1, f32[2,2,96,128]{3,2,1,0:T(8,128)} %constant.6.clone.z_tab_in, f32[5,2,12,128]{3,2,1,0:T(8,128)} %constant.7.clone.y_tab_in, bf16[8,32,16]{2,1,0:T(8,128)(2,1)} %constant.8.clone.x_tab_in, ...), custom_call_target="tpu_custom_call" | custom-call | tf_op jit(solution)/shard_map/chi/pallas_call | solution.py:415
  78.2 1.7 %copy.11 = f32[80,960]{1,0:T(8,128)} copy(f32[80,960]{1,0:T(8,128)} %chi.1) | data formatting | bytes 614400

commit v5 on v0

v5 whole, which is shorter than its diff:
```python
import heapq
import math

import jax
import jax.numpy as jnp
import numpy as np
from jax import lax
from jax.experimental import pallas as pl
from jax.experimental.pallas import tpu as pltpu
from jax.sharding import Mesh
from jax.sharding import PartitionSpec as P

N = 96
RAD = 12
KG = 3840
NV = 16
PLANES = 12
PART = 1152
QUARTER = 240
SUB = 256
MESH_AXES = ("y", "x", "zl", "core", "zh")
SIDE = pl.DeviceIdType.MESH
scope = jax.named_scope


def phase_of(n):
    return 2 * np.pi * np.mod(n, N) / N


def tables():
    j = np.zeros((4, 128), np.int64)
    k = np.zeros((4, 128), np.int64)
    used = np.zeros((4, 2, 128))
    for l in range(91):
        j[0, l], k[0, l] = (-8 + 8 * (l // 13), l % 13) if l < 39 else (-12 + 8 * ((l - 39) // 13), (l - 39) % 13)
        used[0, 0 if l < 39 else 1, l] = 1
    for c in (1, 2, 3):
        for l in range(75):
            j[c, l], k[c, l] = c - 8 + 8 * (l // 25), l % 25 - 12
            used[c, :, l] = 1
    kz = phase_of(np.arange(N)[None, :, None] * k[:2, None, :])
    z_tab = np.stack([np.cos(kz), np.sin(kz)], 1).astype(np.float32)
    jy = phase_of(np.arange(12)[None, :, None] * j[:, None, :])
    waves = np.stack([np.cos(jy), np.sin(jy)], 1)
    first = np.where(used[:, 0, None, None, :] > 0, waves, 0.0)
    second = np.where(used[0, 1, None, None, :] > 0, waves[0], 0.0)
    y_tab = np.concatenate([first, second[None]], 0).astype(np.float32)
    ax = phase_of(np.arange(N).reshape(8, 12)[:, :, None] * np.arange(16)[None, None, :])
    x_tab = np.zeros((8, 32, 16), np.float32)
    x_tab[:, :12] = np.cos(ax)
    x_tab[:, 16:28] = np.sin(ax)
    return z_tab, y_tab, x_tab


def build_waves(t, z_tab, y_tab, tab):
    cz = z_tab[min(t, 1), 0]
    sz = z_tab[min(t, 1), 1]
    for y in range(12):
        row = slice(y * N, (y + 1) * N)
        below = slice(PART + y * N, PART + (y + 1) * N)
        cy = y_tab[t, 0, y : y + 1]
        sy = y_tab[t, 1, y : y + 1]
        co = (cy * cz - sy * sz).astype(jnp.bfloat16)
        si = (sy * cz + cy * sz).astype(jnp.bfloat16)
        tab[t, row, 0:128] = co
        tab[t, row, 128:256] = si
        if t == 0:
            cy = y_tab[4, 0, y : y + 1]
            sy = y_tab[4, 1, y : y + 1]
            tab[t, below, 0:128] = (cy * cz - sy * sz).astype(jnp.bfloat16)
            tab[t, below, 128:256] = (sy * cz + cy * sz).astype(jnp.bfloat16)
        else:
            tab[t, below, 0:128] = -si
            tab[t, below, 128:256] = co


def build_keys(gvec, keys):
    keys[...] = jnp.zeros_like(keys)
    for b in range(16):
        lanes = pl.ds(QUARTER * b, QUARTER)
        a = gvec[0:1, lanes]
        j = gvec[1:2, lanes]
        k = gvec[2:3, lanes]
        j8 = j & 7
        flip = (j8 >= 5) | (((j8 & 3) == 0) & ((k < 0) | ((k == 0) & (j < 0))))
        j = jnp.where(flip, -j, j)
        k = jnp.where(flip, -k, k)
        c = j & 7
        odd = 128 * c + 25 * ((j + 8 - c) >> 3) + k + 12
        even = jnp.where(c == 0, 13 * ((j + 8) >> 3) + k, 39 + 13 * ((j + 12) >> 3) + k)
        lanes = pl.ds(SUB * (b % 4), QUARTER)
        keys[b // 4, 0:1, lanes] = jnp.where((c & 3) == 0, even, odd)
        keys[b // 4, 1:2, lanes] = a
        keys[b // 4, 2:3, lanes] = flip.astype(jnp.int32)


def mix_planes(first, last, vbuf, cbuf, wide, mixed):
    half = jnp.asarray(math.sqrt(0.5), jnp.bfloat16)

    def mix(x, _):
        wide[x] = cbuf[x].astype(jnp.float32)
        for c in range(2):
            row = pl.ds(pl.multiple_of(x * 32 + 16 * c, 16), 16)
            for w in range(0, PART, 384):
                d = []
                for q in range(8):
                    lanes = pl.ds(q * PART + w, 384)
                    band = jnp.broadcast_to(wide[x, c : c + 1, lanes], (16, 384)).astype(jnp.bfloat16)
                    d.append(vbuf[x, :, lanes] * band)
                a = [d[q] + d[q + 4] for q in range(4)]
                m = [d[q] - d[q + 4] for q in range(4)]
                p = (m[1] - m[3]) * half
                r = (m[1] + m[3]) * half
                even = a[0] + a[2]
                odd = a[1] + a[3]
                sums = [(even + odd, even - odd), (m[0] + p, m[2] + r), (a[0] - a[2], a[1] - a[3]), (m[0] - p, r - m[2])]
                for t, (u, v) in enumerate(sums):
                    mixed[t, row, w : w + 384] = u
                    mixed[t, row, PART + w : PART + w + 384] = v
        return 0

    lax.fori_loop(first, last, mix, 0)


def plane_sums(t, mixed, tab, sec):
    both = jnp.dot(mixed[t], tab[t], preferred_element_type=jnp.float32)
    for part in range(2):
        values = both[:, 128 * part : 128 * (part + 1)].astype(jnp.bfloat16)
        sec[:, part, :, 128 * t : 128 * (t + 1)] = values.reshape(PLANES, 32, 128)


def pick(b, q, parts, x_tab, sec, keys):
    lanes = pl.ds(SUB * q, SUB)
    sign = 1.0 - 2.0 * keys[b, 2:3, lanes].astype(jnp.float32)
    hot = (lax.broadcasted_iota(jnp.int32, (512, SUB), 0) == keys[b, 0:1, lanes]).astype(jnp.float32).astype(jnp.bfloat16)
    hot_a = (lax.broadcasted_iota(jnp.int32, (16, SUB), 0) == keys[b, 1:2, lanes]).astype(jnp.float32).astype(jnp.bfloat16)
    wave = jnp.dot(x_tab[...], hot_a, preferred_element_type=jnp.float32)
    got = jnp.dot(sec[...].reshape(64 * PLANES, 512), hot, preferred_element_type=jnp.float32)
    re = jnp.zeros((32, SUB), jnp.float32)
    im = jnp.zeros((32, SUB), jnp.float32)
    for x in range(PLANES):
        co = wave[x : x + 1]
        si = wave[16 + x : 17 + x]
        g_re = got[64 * x : 64 * x + 32]
        g_im = got[64 * x + 32 : 64 * x + 64]
        re += co * g_re - (si * sign) * g_im
        im += si * g_re + (co * sign) * g_im
    parts[b // 2, lax.rem(b, 2), q] = re.astype(parts.dtype)
    parts[2 + b // 2, lax.rem(b, 2), q] = (-im).astype(parts.dtype)


def pair_factor(val_energy, cond_energy, occupation):
    first = ((lax.axis_index("y") * 4 + lax.axis_index("x")) * 3 + lax.axis_index("zh")) * 2
    row = lax.broadcasted_iota(jnp.int32, (32, 16), 0)
    at_v = lax.broadcasted_iota(jnp.int32, (32, 16), 1) == (row & 15)
    ev = jnp.sum(jnp.where(at_v, val_energy, 0.0), axis=1, keepdims=True)
    occ = jnp.sum(jnp.where(at_v, occupation.astype(jnp.float32), 0.0), axis=1, keepdims=True)
    row = lax.broadcasted_iota(jnp.int32, (32, 192), 0)
    at_c = lax.broadcasted_iota(jnp.int32, (32, 192), 1) == first + (row >> 4)
    ec = jnp.sum(jnp.where(at_c, cond_energy, 0.0), axis=1, keepdims=True)
    return jnp.sqrt(occ / (4.0 * (ec - ev))) * (1.0 / N**1.5)


EARLY = 8
CHAINED = 20


def step_of(way, hop):
    return 4 if hop == 4 else -way * hop


def carried(way, hop):
    return (0, 1) if hop < 4 else ((0,) if way == 1 else (1,))


RING = [(t, way, hop, h) for t in range(3) for way in (1, -1) for hop in (1, 2, 3, 4) for h in carried(way, hop)]
RING_AT = {piece: i for i, piece in enumerate(RING)}


def timetable(zh):
    ready = (0.0, 2.3, 4.6)
    queue = []
    for h in range(2):
        heapq.heappush(queue, (ready[zh] + 0.42 * h, 0, ("own", h)))
        for t in (1, 2):
            there = max(ready[(zh - t) % 3] + 6.84, ready[zh] + 1.87)
            heapq.heappush(queue, (there + 2.62 * h, 1, ("zh", t, h)))
    free = {1: 0.0, -1: 0.0}
    left = {(t, step): 2 for t in range(3) for step in range(-3, 5)}
    slot = {}
    order = []

    def send(now, t, way, hop, h):
        free[way] = max(free[way], now) + 0.96
        heapq.heappush(queue, (free[way] + 4.43, 2, ("ring", t, way, hop, h)))

    def have(now, t, step):
        left[t, step] -= 1
        if not left[t, step]:
            slot[t, step] = len(slot)
            heapq.heappush(queue, (now, 3, ("give", t, step)))
            for far in (1, 2, 3) if slot[t, step] < CHAINED else (1,):
                heapq.heappush(queue, (now + 3.67 + 3.14 * far, 4, ("relay", t, step, far)))

    while queue:
        now, _, event = heapq.heappop(queue)
        order.append(event)
        if event[0] in ("own", "zh"):
            t, h = (0, event[1]) if event[0] == "own" else event[1:]
            for way in (1, -1):
                send(now, t, way, 1, h)
            have(now, t, 0)
        elif event[0] == "ring":
            _, t, way, hop, h = event
            if hop < 4 and h in carried(way, hop + 1):
                send(now, t, way, hop + 1, h)
            have(now, t, step_of(way, hop))
    return order, slot


TABLES = [timetable(zh) for zh in range(3)]


def turned(axis, step):
    size = lax.axis_size(axis)
    return lax.rem(lax.axis_index(axis) + step % size, size)


def remote(src, dst, send_sem, recv_sem, target):
    return pltpu.make_async_remote_copy(
        src_ref=src, dst_ref=dst, send_sem=send_sem, recv_sem=recv_sem, device_id=target, device_id_type=SIDE
    )


def chi_body(
    val, con, gvec_in, z_in_tab, y_in_tab, x_in_tab, val_energy_in, cond_energy_in, occupation_in, out,
    val_energy, cond_energy, occupation, gvec, z_tab, y_tab, x_tab, vbuf, cbuf, wide, tab, mixed, sec, keys,
    parts, core_in, z_out, z_in, cols, rows, left, sums, far_out, far_in, x_out, x_in,
    small_sems, load_sems, core_sems, z_sems, zh_sems, y_sems, row_sems, far_sems, x_sems, out_sems,
):
    y, x, zl, core, zh = (lax.axis_index(a) for a in MESH_AXES)
    grow = 2 * zl + core
    loads = [
        [pltpu.make_async_copy(a.at[pl.ds(3 * s, 3)], b.at[pl.ds(3 * s, 3)], load_sems.at[i, s]) for i, (a, b) in enumerate([(val, vbuf), (con, cbuf)])]
        for s in range(4)
    ]
    small = [
        pltpu.make_async_copy(a, b, small_sems.at[i])
        for i, (a, b) in enumerate([
            (gvec_in, gvec), (z_in_tab, z_tab), (y_in_tab, y_tab), (x_in_tab.at[grow], x_tab),
            (val_energy_in, val_energy), (cond_energy_in, cond_energy), (occupation_in, occupation),
        ])
    ]
    for c in small[:1] + [c for pair in loads for c in pair] + small[1:]:
        c.start()

    barrier = pltpu.get_barrier_semaphore()
    other = {"core": 1 - core}
    partners = [other] + [{"zl": turned("zl", k)} for k in (1, 2, 3)] + [{"zh": turned("zh", k)} for k in (1, 2)]
    partners += [{"y": turned("y", k)} for k in (1, 7)] + [{"x": turned("x", k)} for k in (1, 3)]
    for target in partners:
        pl.semaphore_signal(barrier, inc=1, device_id=target, device_id_type=SIDE)

    with scope("keys"):
        small[0].wait()
        build_keys(gvec, keys)
    with scope("mix"):
        for s in range(4):
            for c in loads[s]:
                c.wait()
            mix_planes(3 * s, 3 * s + 3, vbuf, cbuf, wide, mixed)
    for c in small[1:]:
        c.wait()
    with scope("planes"):
        build_waves(0, z_tab, y_tab, tab)
        for t in range(4):
            if t < 3:
                build_waves(t + 1, z_tab, y_tab, tab)
            plane_sums(t, mixed, tab, sec)
        factor = pair_factor(val_energy[...], cond_energy[...], occupation[...])
    with scope("barrier"):
        pl.semaphore_wait(barrier, len(partners))

    odd = 1 - lax.rem(zl, 2)

    def swap(k, q):
        return remote(parts.at[turned("zl", k), 1 - core, q], core_in.at[q, k], out_sems.at[0], core_sems.at[q], other)

    def pass_on(k, q):
        return remote(z_out.at[q, k - 1], z_in.at[q, k - 1], out_sems.at[1], z_sems.at[q], {"zl": turned("zl", k)})

    def both_cores(k, q):
        return parts[turned("zl", k), core, q].astype(jnp.float32) + core_in[q, k].astype(jnp.float32)

    def combine(q):
        remote(core_in.at[q], core_in.at[q], out_sems.at[0], core_sems.at[q], other).wait_recv()
        for k in (2, 1, 3):
            z_out[q, k - 1] = both_cores(k, q).astype(jnp.bfloat16)
            pass_on(k, q).start()

    for q in range(4):
        with scope("pick%d" % q):
            for block in (2 * odd + 1 - core, 3 - core - 2 * odd, 2 * odd + core, 2 - 2 * odd + core):
                pick(block, q, parts, x_tab, sec, keys)
            for k in (1, 3, 2, 0):
                swap(k, q).start()
        if q:
            with scope("combine%d" % (q - 1)):
                combine(q - 1)
    with scope("combine3"):
        combine(3)

    home = y // 2
    on_chain = core == lax.rem(y, 2)
    source = on_chain & (zl == home)

    def row_copy(s, i, target):
        return remote(rows.at[s], rows.at[s], out_sems.at[6 + i], row_sems.at[s], target)

    def along(s, first):
        @pl.when((zl < 3) & ((zl > home) | first))
        def _():
            row_copy(s, 1, {"zl": turned("zl", 1)}).start()

        @pl.when((zl > 0) & ((zl < home) | first))
        def _():
            row_copy(s, 2, {"zl": turned("zl", 3)}).start()

    def rows_here(first, last):
        @pl.when(jnp.logical_not(on_chain))
        def _():
            for s in range(first, last):
                row_copy(s, 0, other).wait_recv()

    def through(q):
        return remote(far_out.at[q], far_in.at[q], out_sems.at[4], far_sems.at[q], {"x": turned("x", 1 if q < 2 else 3)})

    def send_sum(side, q):
        return remote(x_out.at[side, q], x_in.at[side, q], out_sems.at[5], x_sems.at[side, q], {"x": turned("x", 3 if side else 1)})

    def group_of(k, q):
        return sums[q, pl.ds(pl.multiple_of(80 * turned("x", k), 80), 80)]

    def product(q, first, last):
        pairs = slice(32 * first, 32 * last)
        right = cols[q // 2, first:last, :, SUB * (q % 2) : SUB * (q % 2 + 1)].reshape(32 * (last - first), SUB)
        return jnp.dot(left[:, pairs], right, preferred_element_type=jnp.float32)

    def turn(first, last):
        left[:, 32 * first : 32 * last] = rows[first:last, :, 0:320].reshape(32 * (last - first), 320).T

    def gather(third):
        order, slot = TABLES[third]

        def to_gcol(k, h):
            return remote(cols.at[h, slot[0, 0]], cols.at[h, TABLES[(third + k) % 3][1][k, 0]], out_sems.at[2], zh_sems.at[k - 1, h], {"zh": turned("zh", k)})

        def ring(t, way, hop, h):
            held = slot[t, step_of(way, hop - 1) if hop > 1 else 0]
            return remote(cols.at[h, held], cols.at[h, slot[t, step_of(way, hop)]], out_sems.at[3], y_sems.at[RING_AT[t, way, hop, h]], {"y": turned("y", way)})

        def give(t, step):
            s = slot[t, step]

            @pl.when(source)
            def _():
                for q in range(4):
                    at = SUB * (q % 2) + 80 * third
                    rows[s, :, 80 * q : 80 * q + 80] = cols[q // 2, s, :, at : at + 80]

                if s < CHAINED:
                    along(s, True)
                else:
                    for k in (3, 2, 1):
                        row_copy(s, 3, {"zl": turned("zl", k)}).start()
                row_copy(s, 0, other).start()

        def relay(t, step, far):
            s = slot[t, step]
            away = (zl != home) if s >= CHAINED else ((zl == home + far) | (zl == home - far))

            @pl.when(on_chain & away)
            def _():
                row_copy(s, 0, other).wait_recv()
                if s < CHAINED and far < 3:
                    along(s, False)
                row_copy(s, 0, other).start()

        def handle(event):
            kind = event[0]
            if kind == "own":
                h = event[1]
                with scope("own%d" % h):
                    for q in (2 * h, 2 * h + 1):
                        remote(z_in.at[q], z_in.at[q], out_sems.at[1], z_sems.at[q], other).wait_recv()
                        total = both_cores(0, q)
                        for k in range(3):
                            total += z_in[q, k].astype(jnp.float32)
                        cols[h, slot[0, 0], :, SUB * (q % 2) : SUB * (q % 2 + 1)] = (total * factor).astype(jnp.bfloat16)
                for k in (1, 2):
                    to_gcol(k, h).start()
                for way in (1, -1):
                    ring(0, way, 1, h).start()
            elif kind == "zh":
                _, t, h = event
                with scope("zh%d%d" % (t, h)):
                    to_gcol(t, h).wait_recv()
                for way in (1, -1):
                    ring(t, way, 1, h).start()
            elif kind == "ring":
                _, t, way, hop, h = event
                with scope("ring%d%d%d%d" % (t, max(way, 0), hop, h)):
                    ring(t, way, hop, h).wait_recv()
                if hop < 4 and h in carried(way, hop + 1):
                    ring(t, way, hop + 1, h).start()
            elif kind == "give":
                give(*event[1:])
            else:
                relay(*event[1:])

        until = max(i for i, event in enumerate(order) if event[0] == "relay" and slot[event[1:3]] < EARLY) + 1
        for event in order[:until]:
            handle(event)
        with scope("early"):
            rows_here(0, EARLY)
            turn(0, EARLY)
            for q in range(4):
                sums[q] = product(q, 0, EARLY)
        for event in order[until:]:
            handle(event)

    for third in range(3):

        @pl.when(zh == third)
        def _():
            gather(third)

    with scope("rows"):
        rows_here(EARLY, 24)
    with scope("matmul"):
        turn(EARLY, 24)
        for q in range(4):
            sums[q] = sums[q] + product(q, EARLY, 24)
            far_out[q] = group_of(2, q).astype(jnp.bfloat16)
            through(q).start()
            side = 1 if q < 2 else 0
            x_out[side, q] = group_of(3 if side else 1, q).astype(jnp.bfloat16)
            send_sum(side, q).start()
    with scope("xpass"):
        for q in (0, 2, 1, 3):
            side = 0 if q < 2 else 1
            through(q).wait_recv()
            x_out[side, q] = (group_of(3 if side else 1, q) + far_in[q].astype(jnp.float32)).astype(jnp.bfloat16)
            send_sum(side, q).start()
    for q in (0, 2, 1, 3):
        with scope("xsum%d" % q):
            total = group_of(0, q)
            for side in ((1, 0) if q < 2 else (0, 1)):
                send_sum(side, q).wait_recv()
                total += x_in[side, q].astype(jnp.float32)
            out[:, QUARTER * q : QUARTER * (q + 1)] = total[:, :QUARTER]

    def gone(ref, i):
        remote(ref, ref, out_sems.at[i], far_sems.at[0], other).wait_send()

    with scope("gone"):
        gone(core_in, 0)
        gone(z_in, 1)
        gone(cols.at[:, 0:2], 2)
        gone(cols.at[:, 0:21], 3)
        gone(far_in, 4)
        gone(x_in, 5)

        @pl.when(on_chain)
        def _():
            gone(rows, 6)

        @pl.when(on_chain & (zl < 3) & (zl >= home))
        def _():
            gone(rows.at[0:CHAINED], 7)

        @pl.when(on_chain & (zl > 0) & (zl <= home))
        def _():
            gone(rows.at[0:CHAINED], 8)

        @pl.when(source)
        def _():
            gone(rows.at[0 : 3 * (24 - CHAINED)], 9)


def scratch():
    dma = pltpu.SemaphoreType.DMA
    bf = jnp.bfloat16
    f32 = jnp.float32
    return [
        pltpu.VMEM((1, NV), f32), pltpu.VMEM((1, 192), f32), pltpu.VMEM((1, NV), jnp.int32),
        pltpu.VMEM((3, KG), jnp.int32), pltpu.VMEM((2, 2, N, 128), f32), pltpu.VMEM((5, 2, 12, 128), f32), pltpu.VMEM((32, 16), bf),
        pltpu.VMEM((PLANES, NV, N * N), bf), pltpu.VMEM((PLANES, 2, N * N), bf), pltpu.VMEM((PLANES, 2, N * N), f32),
        pltpu.VMEM((4, 2 * PART, 256), bf), pltpu.VMEM((4, 384, 2 * PART), bf), pltpu.VMEM((PLANES, 2, 32, 512), bf), pltpu.VMEM((4, 8, 4 * SUB), jnp.int32),
        pltpu.VMEM((4, 2, 4, 32, SUB), bf), pltpu.VMEM((4, 4, 32, SUB), bf), pltpu.VMEM((4, 3, 32, SUB), bf), pltpu.VMEM((4, 3, 32, SUB), bf),
        pltpu.VMEM((2, 24, 32, 2 * SUB), bf), pltpu.VMEM((24, 32, 384), bf), pltpu.VMEM((320, 768), bf), pltpu.VMEM((4, 320, SUB), f32), pltpu.VMEM((4, 80, SUB), bf), pltpu.VMEM((4, 80, SUB), bf), pltpu.VMEM((2, 4, 80, SUB), bf), pltpu.VMEM((2, 4, 80, SUB), bf),
        dma((7,)), dma((2, 4)), dma((4,)), dma((4,)), dma((2, 2)), dma((len(RING),)), dma((24,)), dma((4,)), dma((2, 4)), dma((10,)),
    ]


def body(valence, conduction, val_energy, cond_energy, val_occupation, gvectors):
    z_tab, y_tab, x_tab = tables()
    chi = pl.pallas_call(
        chi_body,
        out_shape=pltpu.VMEM((80, 4 * QUARTER), jnp.float32),
        in_specs=[pl.BlockSpec(memory_space=pl.ANY)] * 9,
        out_specs=pl.BlockSpec(memory_space=pltpu.VMEM),
        scratch_shapes=scratch(),
        compiler_params=pltpu.CompilerParams(collective_id=0, has_side_effects=True, vmem_limit_bytes=60 * 2**20),
        name="chi",
    )(
        valence.transpose(1, 0, 2), conduction.transpose(1, 0, 2), gvectors,
        jnp.asarray(z_tab), jnp.asarray(y_tab), jnp.asarray(x_tab, jnp.bfloat16),
        val_energy.reshape(1, NV), cond_energy.reshape(1, 192), val_occupation.reshape(1, NV),
    )
    return chi * (-1.0 / math.sqrt(3072))


def solution(mesh):
    finer = Mesh(mesh.devices.reshape(8, 4, 4, 2, 3), MESH_AXES)
    grow = ("zl", "core")
    bands = ("y", "x", "zh")
    placed = (P(None, grow, None), P(bands, grow, None), P(), P(), P(), P())
    return jax.shard_map(body, mesh=finer, in_specs=placed, out_specs=P(bands, grow), check_vma=False)
```

time: 238 us -> 66.7 us (0.28)
  the two profiles are of different devices: /device:TPU:2 before, /device:TPU:48 now
where the time goes in v5:
time: 66.7 us; the launch traced here: 66.3 us
  Pallas kernels  65.5 us (98%)
  other arithmetic  0.76 us (1%)
    pallas_call x1, Pallas kernels, body(): pl.pallas_call(chi_body, out_shape=pltpu.VMEM((80, 4 * QUARTER), jnp.floa...  65.5 us

profile of v5, /device:TPU:48, one launch (start us, length us, event | category | flops | bytes accessed | tf_op | source)
XLA Modules:
  0.0 66.3 jit_solution(6482126764436941519)
XLA Ops:
  0.0 65.5 %chi.1 = f32[80,960]{1,0:T(8,128)S(1)} custom-call(bf16[12,16,9216]{2,1,0:T(8,128)(2,1)} %bitcast.5, bf16[12,2,9216]{2,1,0:T(2,128)(2,1)} %bitcast.6, s32[3,3840]{1,0:T(4,128)} %gvec_in.1, f32[2,2,96,128]{3,2,1,0:T(8,128)} %constant.8.clone.z_in_tab, f32[5,2,12,128]{3,2,1,0:T(8,128)} %constant.9.clone.y_in_tab, bf16[8,32,16]{2,1,0:T(8,128)(2,1)} %constant.10.clone.x_in_tab, ...), custom_call_target="tpu_custom_call" | custom-call | tf_op jit(solution)/shard_map/chi/pallas_call | solution.py:508
  65.5 0.8 %broadcast_multiply_fusion = f32[80,960]{1,0:T(8,128)} fusion(f32[80,960]{1,0:T(8,128)S(1)} %chi.1), kind=kLoop, calls=%fused_computation | loop fusion | flops 76800 | bytes 614400 | tf_op jit(solution)/shard_map/mul | solution.py:521
